TPU v7x, 8 devices: a whole 2x2x1 slice. The times are simulated.
8 devices in a mesh: dp: 2 (over z, y), sp: 4 (over x, core).
Axes of the slice: x: 2, y: 2, z: 1, core: 2. Of those that a mesh axis runs over, the one named last changes fastest.
Arguments:
- hidden: bfloat16 [8192, 1536], P(('dp', 'sp')), parts along dimension 0
- positions: int32 [8192], P(('dp', 'sp')), parts along dimension 0
- attn_gain: bfloat16 [1536], replicated
- w_query: bfloat16 [1536, 1536], replicated
- w_key: bfloat16 [1536, 256], replicated
- w_value: bfloat16 [1536, 256], replicated
- w_out: bfloat16 [1536, 1536], replicated
- mlp_gain: bfloat16 [1536], replicated
- w_gate: bfloat16 [1536, 8960], replicated
- w_up: bfloat16 [1536, 8960], replicated
- w_down: bfloat16 [8960, 1536], replicated
Outputs:
- output 1: bfloat16 [8192, 1536], P(('dp', 'sp')), parts along dimension 0
- output 2: bfloat16 [8192, 4, 128], P('dp', 'sp'), parts along dimension 0
- output 3: bfloat16 [8192, 4, 128], P('dp', 'sp'), parts along dimension 0
There are 2 independent parts. A program takes and returns all parts, laid end to end along the dimension named above; an argument that names none is the same for every part.
All inputs are finite; a program needn't handle non-finite values.
Results may differ from a plain program's by a relative error of at most 0.00947955.
Values are sent between devices in bfloat16 or wider.
A program may use at most 1 GiB of HBM per device.

v0:
```python
import jax
import jax.numpy as jnp
from jax import lax
from jax.sharding import PartitionSpec as P

HEAD_DIM = 128
ROPE_THETA = 500000
NORM_EPS = 1e-5
BLOCK_LEN = 512


def rms_norm(acts_in, gain_vec):
    rows_f32 = acts_in.astype(jnp.float32)
    mean_sq = jnp.mean(rows_f32 * rows_f32, axis=-1, keepdims=True)
    return (rows_f32 * lax.rsqrt(mean_sq + NORM_EPS) * gain_vec.astype(jnp.float32)).astype(jnp.bfloat16)


def rotary(heads_in, positions):
    half_dim = HEAD_DIM // 2
    inv_freq = 1.0 / (ROPE_THETA ** (jnp.arange(0, HEAD_DIM, 2, dtype=jnp.float32) / HEAD_DIM))
    angles = positions.astype(jnp.float32)[:, None] * inv_freq[None, :]
    cos_part = jnp.cos(angles)[:, None, :]
    sin_part = jnp.sin(angles)[:, None, :]
    first_half = heads_in[..., :half_dim]
    second_half = heads_in[..., half_dim:]
    return jnp.concatenate([first_half * cos_part - second_half * sin_part, second_half * cos_part + first_half * sin_part], axis=-1)


def causal_attention(q_grp, k_all, v_all, key_ok, q_base):
    q_len, kv_local, group_rep, head_dim = q_grp.shape
    block_len = min(BLOCK_LEN, q_len)
    num_qblocks = q_len // block_len
    score_scale = head_dim ** -0.5
    q_blocks = q_grp.reshape(num_qblocks, block_len, kv_local, group_rep, head_dim)
    offsets = jnp.arange(block_len)

    def one_block(block_args):
        q_blk, block_idx = block_args
        q_start = q_base + block_idx * block_len
        q_idx = q_start + offsets

        def kv_step(kv_idx, run_state):
            run_max, run_sum, acc_pv = run_state
            k_start = kv_idx * block_len
            k_blk = lax.dynamic_slice_in_dim(k_all, k_start, block_len, 0)
            v_blk = lax.dynamic_slice_in_dim(v_all, k_start, block_len, 0)
            ok_blk = lax.dynamic_slice_in_dim(key_ok, k_start, block_len, 0)
            k_idx = k_start + offsets
            allowed = (k_idx[None, :] <= q_idx[:, None]) & ok_blk[None, :]
            scores = jnp.einsum("qgrd,kgd->qgrk", q_blk, k_blk, preferred_element_type=jnp.float32) * score_scale
            scores = jnp.where(allowed[:, None, None, :], scores, -jnp.inf)
            new_max = jnp.maximum(run_max, jnp.max(scores, axis=-1))
            safe_max = jnp.where(jnp.isfinite(new_max), new_max, 0.0)
            weights = jnp.exp(scores - safe_max[..., None])
            decay_fac = jnp.exp(run_max - safe_max)
            run_sum = run_sum * decay_fac + jnp.sum(weights, axis=-1)
            acc_pv = acc_pv * decay_fac[..., None] + jnp.einsum("qgrk,kgd->qgrd", weights.astype(jnp.bfloat16), v_blk, preferred_element_type=jnp.float32)
            return new_max, run_sum, acc_pv

        init_state = (jnp.full((block_len, kv_local, group_rep), -jnp.inf, jnp.float32), jnp.zeros((block_len, kv_local, group_rep), jnp.float32), jnp.zeros((block_len, kv_local, group_rep, head_dim), jnp.float32))
        num_steps = q_start // block_len + 1
        final_max, final_sum, final_acc = lax.fori_loop(0, num_steps, kv_step, init_state)
        return (final_acc / jnp.where(final_sum > 0, final_sum, 1.0)[..., None]).astype(jnp.bfloat16)

    attn_blocks = lax.map(one_block, (q_blocks, jnp.arange(num_qblocks)))
    return attn_blocks.reshape(q_len, kv_local, group_rep, head_dim)


def solution(mesh):
    groups = mesh.shape["sp"]

    def layer_shard(hidden, positions, attn_gain, w_query, w_key, w_value, w_out, mlp_gain, w_gate, w_up, w_down):
        tok_rows = hidden.shape[0]
        heads = w_query.shape[1] // HEAD_DIM
        kv_heads = w_key.shape[1] // HEAD_DIM
        cache_slots = max(kv_heads, groups)
        kv_local = cache_slots // groups
        copies = cache_slots // kv_heads
        heads_local = heads // groups
        h_norm = rms_norm(hidden, attn_gain)
        q_rot = rotary(jnp.dot(h_norm, w_query, preferred_element_type=jnp.float32).reshape(tok_rows, heads, HEAD_DIM), positions).astype(jnp.bfloat16)
        k_rot = rotary(jnp.dot(h_norm, w_key, preferred_element_type=jnp.float32).reshape(tok_rows, kv_heads, HEAD_DIM), positions).astype(jnp.bfloat16)
        v_proj = jnp.dot(h_norm, w_value, preferred_element_type=jnp.float32).astype(jnp.bfloat16).reshape(tok_rows, kv_heads, HEAD_DIM)
        slot_shape = (tok_rows, kv_heads, copies, HEAD_DIM)
        k_slots = jnp.broadcast_to(k_rot[:, :, None, :], slot_shape).reshape(tok_rows, cache_slots, HEAD_DIM)
        v_slots = jnp.broadcast_to(v_proj[:, :, None, :], slot_shape).reshape(tok_rows, cache_slots, HEAD_DIM)
        q_heads = lax.all_to_all(q_rot, "sp", 1, 0, tiled=True)
        k_heads = lax.all_to_all(k_slots, "sp", 1, 0, tiled=True)
        v_heads = lax.all_to_all(v_slots, "sp", 1, 0, tiled=True)
        pos_all = lax.all_gather(positions, "sp", axis=0, tiled=True)
        seq_len = q_heads.shape[0]
        q_grp = q_heads.reshape(seq_len, kv_local, heads_local // kv_local, HEAD_DIM)
        attn_heads = causal_attention(q_grp, k_heads, v_heads, pos_all >= 0, 0).reshape(seq_len, heads_local, HEAD_DIM)
        attn_tok = lax.all_to_all(attn_heads, "sp", 0, 1, tiled=True).reshape(tok_rows, heads * HEAD_DIM)
        x_mid = (hidden.astype(jnp.float32) + jnp.dot(attn_tok, w_out, preferred_element_type=jnp.float32)).astype(jnp.bfloat16)
        g_norm = rms_norm(x_mid, mlp_gain)
        gate_proj = jnp.dot(g_norm, w_gate, preferred_element_type=jnp.float32)
        up_proj = jnp.dot(g_norm, w_up, preferred_element_type=jnp.float32)
        act_mix = (jax.nn.silu(gate_proj) * up_proj).astype(jnp.bfloat16)
        hidden_out = (x_mid.astype(jnp.float32) + jnp.dot(act_mix, w_down, preferred_element_type=jnp.float32)).astype(jnp.bfloat16)
        return hidden_out, k_heads, v_heads

    row_spec = P(("dp", "sp"), None)
    cache_spec = P("dp", "sp", None)
    return jax.shard_map(layer_shard, mesh=mesh, in_specs=(row_spec, P(("dp", "sp")), P(), P(), P(), P(), P(), P(), P(), P(), P()), out_specs=(row_spec, cache_spec, cache_spec), check_vma=False)
```

profile of v0, /device:TPU:0, one launch (start us, length us, event | category | flops | bytes accessed | tf_op | source)
XLA Modules:
  0.0 429.3 jit_solution(2646398357057124070)
XLA Ops:
  0.7 2.7 fusion.33
  3.7 1.3 convolution_convert_fusion
  6.5 4.6 %all-to-all-start.2 = ((bf16[1024,4,128]{2,0,1:T(8,128)(2,1)}), bf16[1024,4,128]{2,0,1:T(8,128)(2,1)S(1)}, u32[]{:S(2)}, u32[]{:S(2)}) async-start(bf16[1024,4,128]{2,0,1:T(8,128)(2,1)} %bitcast.25), calls=%async_computation.2 | async-start | bytes 2097152 | tf_op jit(solution)/shard_map/all_to_all | solution.py:89
  11.1 8.5 %fusion.52 = f32[1024,1536]{0,1:T(8,128)S(1)} fusion(bf16[1536,1536]{1,0:T(8,128)(2,1)} %param.18, bf16[1024,1536]{1,0:T(8,128)(2,1)} %param.15, f32[1536]{0:T(1024)S(1)} %convert_element_type.52, f32[1024]{0:T(1024)S(1)} %add_rsqrt_fusion.1), kind=kOutput, calls=%fused_computation.73 | convolution fusion | flops 4838129664 | bytes 14166016 | tf_op jit(solution)/shard_map/dot_general | solution.py:81
  21.7 2.0 pad_maximum_fusion
  23.7 1.6 all-to-all-done.2
  25.3 4.7 %all-to-all-start = ((bf16[1024,12,128]{0,2,1:T(8,128)(2,1)}), bf16[1024,12,128]{0,2,1:T(8,128)(2,1)}, u32[]{:S(2)}, u32[]{:S(2)}) async-start(bf16[1024,12,128]{0,2,1:T(8,128)(2,1)} %pad_maximum_fusion), calls=%async_computation | async-start | bytes 6291456 | tf_op jit(solution)/shard_map/all_to_all | solution.py:87
  30.0 3.1 fusion.50
  33.6 33.0 %all-to-all-done = bf16[1024,12,128]{0,2,1:T(8,128)(2,1)} async-done(((bf16[1024,12,128]{0,2,1:T(8,128)(2,1)}), bf16[1024,12,128]{0,2,1:T(8,128)(2,1)}, u32[]{:S(2)}, u32[]{:S(2)}) %all-to-all-start) | async-done | bytes 3145760 | tf_op jit(solution)/shard_map/all_to_all | solution.py:87
  67.7 3.5 all-to-all-start.1
  71.3 16.5 %all_gather.3 = s32[4096]{0:T(1024)S(1)} all-gather(s32[1024]{0:T(1024)S(1)} %copy-done.7), channel_id=1, replica_groups=mesh['dp'=2,'sp'=4] {'sp'}, dimensions={0}, use_global_device_ids=true | all-gather | bytes 20480 | tf_op jit(solution)/shard_map/all_gather | solution.py:90
  88.3 4.6 %copy.43 = bf16[4,1024,3,128]{3,1,0,2:T(8,128)(2,1)} copy(bf16[4,1024,3,128]{1,3,2,0:T(8,128)(2,1)} %bitcast.17) | data formatting | bytes 6291456 | tf_op jit(solution)/shard_map/all_to_all | solution.py:87
  92.9 140.8 %while.43 = (s32[]{:T(128)}, bf16[8,512,1,3,128]{4,1,0,3,2:T(8,128)(2,1)}, s32[8]{0:T(128)S(1)}, bf16[8,512,1,3,128]{4,1,0,3,2:T(8,128)(2,1)}, pred[4096]{0:T(10...) while((s32[]{:T(128)}, ...), condition=%wide.region_6.7_spmd.clone.clone, body=%wide.region_1.6_spmd.clone.clone.sunk | while | flops 412632608 | bytes 17199312 | solution.py:65
  95.5 3.1 while.44
  97.3 1.2 fusion.87
  102.3 6.2 %while.44 = (s32[]{:T(128)}, f32[512,1,3]{0,2,1:T(4,128)S(1)}, f32[512,1,3]{0,2,1:T(4,128)S(1)}, f32[512,1,3,128]{0,3,2,1:T(8,128)S(1)}, s32[]{:T(128)}, /*index...) while((s32[]{:T(128)}, f32[512,1,3]{0,2,1:T(4,128)S(1)}, ...), condition=%wide.region_5.5_spmd, body=%wide.region_2.4_spmd.sunk | while | flops 412235776 | bytes 12838603 | solution.py:62
  104.1 1.2 fusion.87
  107.1 1.2 fusion.87
  112.1 9.2 %while.44 = (s32[]{:T(128)}, f32[512,1,3]{0,2,1:T(4,128)S(1)}, f32[512,1,3]{0,2,1:T(4,128)S(1)}, f32[512,1,3,128]{0,3,2,1:T(8,128)S(1)}, s32[]{:T(128)}, /*index...) while((s32[]{:T(128)}, f32[512,1,3]{0,2,1:T(4,128)S(1)}, ...), condition=%wide.region_5.5_spmd, body=%wide.region_2.4_spmd.sunk | while | flops 412235776 | bytes 12838603 | solution.py:62
  113.9 1.2 fusion.87
  117.0 1.2 fusion.87
  120.1 1.2 fusion.87
  125.1 12.3 %while.44 = (s32[]{:T(128)}, f32[512,1,3]{0,2,1:T(4,128)S(1)}, f32[512,1,3]{0,2,1:T(4,128)S(1)}, f32[512,1,3,128]{0,3,2,1:T(8,128)S(1)}, s32[]{:T(128)}, /*index...) while((s32[]{:T(128)}, f32[512,1,3]{0,2,1:T(4,128)S(1)}, ...), condition=%wide.region_5.5_spmd, body=%wide.region_2.4_spmd.sunk | while | flops 412235776 | bytes 12838603 | solution.py:62
  126.9 1.2 fusion.87
  130.0 1.2 fusion.87
  133.1 1.2 fusion.87
  136.1 1.3 fusion.87
  141.2 15.4 %while.44 = (s32[]{:T(128)}, f32[512,1,3]{0,2,1:T(4,128)S(1)}, f32[512,1,3]{0,2,1:T(4,128)S(1)}, f32[512,1,3,128]{0,3,2,1:T(8,128)S(1)}, s32[]{:T(128)}, /*index...) while((s32[]{:T(128)}, f32[512,1,3]{0,2,1:T(4,128)S(1)}, ...), condition=%wide.region_5.5_spmd, body=%wide.region_2.4_spmd.sunk | while | flops 412235776 | bytes 12838603 | solution.py:62
  142.9 1.2 fusion.87
  146.0 1.3 fusion.87
  149.1 1.2 fusion.87
  152.2 1.3 fusion.87
  155.3 1.2 fusion.87
  160.3 18.5 %while.44 = (s32[]{:T(128)}, f32[512,1,3]{0,2,1:T(4,128)S(1)}, f32[512,1,3]{0,2,1:T(4,128)S(1)}, f32[512,1,3,128]{0,3,2,1:T(8,128)S(1)}, s32[]{:T(128)}, /*index...) while((s32[]{:T(128)}, f32[512,1,3]{0,2,1:T(4,128)S(1)}, ...), condition=%wide.region_5.5_spmd, body=%wide.region_2.4_spmd.sunk | while | flops 412235776 | bytes 12838603 | solution.py:62
  165.2 1.2 fusion.87
  168.3 1.2 fusion.87
  171.3 1.3 fusion.87
  174.4 1.2 fusion.87
  177.5 1.3 fusion.87
  182.5 21.6 %while.44 = (s32[]{:T(128)}, f32[512,1,3]{0,2,1:T(4,128)S(1)}, f32[512,1,3]{0,2,1:T(4,128)S(1)}, f32[512,1,3,128]{0,3,2,1:T(8,128)S(1)}, s32[]{:T(128)}, /*index...) while((s32[]{:T(128)}, f32[512,1,3]{0,2,1:T(4,128)S(1)}, ...), condition=%wide.region_5.5_spmd, body=%wide.region_2.4_spmd.sunk | while | flops 412235776 | bytes 12838603 | solution.py:62
  184.3 1.2 fusion.87
  187.4 1.3 fusion.87
  190.5 1.2 fusion.87
  193.6 1.3 fusion.87
  196.7 1.2 fusion.87
  199.7 1.3 fusion.87
  202.8 1.2 fusion.87
  207.8 24.7 %while.44 = (s32[]{:T(128)}, f32[512,1,3]{0,2,1:T(4,128)S(1)}, f32[512,1,3]{0,2,1:T(4,128)S(1)}, f32[512,1,3,128]{0,3,2,1:T(8,128)S(1)}, s32[]{:T(128)}, /*index...) while((s32[]{:T(128)}, f32[512,1,3]{0,2,1:T(4,128)S(1)}, ...), condition=%wide.region_5.5_spmd, body=%wide.region_2.4_spmd.sunk | while | flops 412235776 | bytes 12838603 | solution.py:62
  212.7 1.2 fusion.87
  215.8 1.2 fusion.87
  218.9 1.3 fusion.87
  222.0 1.2 fusion.87
  225.0 1.3 fusion.87
  228.1 1.2 fusion.87
  231.2 1.3 fusion.87
  233.7 7.2 %copy.49 = bf16[4096,3,128]{2,1,0:T(4,128)(2,1)} copy(bf16[4096,3,128]{2,0,1:T(8,128)(2,1)} %bitcast.136) | data formatting | bytes 6291456 | tf_op jit(solution)/shard_map/reshape;reshape | solution.py:93
  240.9 5.0 %all-to-all-start.3 = ((bf16[4096,3,128]{2,1,0:T(4,128)(2,1)}), bf16[4096,3,128]{2,1,0:T(4,128)(2,1)}, u32[]{:S(2)}, u32[]{:S(2)}) async-start(bf16[4096,3,128]{2,1,0:T(4,128)(2,1)} %copy.49), calls=%async_computation.3 | async-start | bytes 8388608 | tf_op jit(solution)/shard_map/all_to_all | solution.py:94
  245.9 47.9 %all-to-all-done.3 = bf16[4096,3,128]{2,1,0:T(4,128)(2,1)} async-done(((bf16[4096,3,128]{2,1,0:T(4,128)(2,1)}), bf16[4096,3,128]{2,1,0:T(4,128)(2,1)}, u32[]{:S(2)}, u32[]{:S(2)}) %all-to-all-start.3) | async-done | bytes 3145760 | tf_op jit(solution)/shard_map/all_to_all | solution.py:94
  293.7 4.3 %copy.50 = bf16[4096,3,128]{2,0,1:T(8,128)(2,1)} copy(bf16[4096,3,128]{2,1,0:T(4,128)(2,1)} %all-to-all-done.3) | data formatting | bytes 6291456 | tf_op jit(solution)/shard_map/all_to_all | solution.py:94
  298.0 4.7 %copy.51 = bf16[1024,4,3,128]{0,3,2,1:T(8,128)(2,1)} copy(bf16[1024,4,3,128]{3,0,1,2:T(8,128)(2,1)} %bitcast.131) | data formatting | bytes 6291456 | tf_op jit(solution)/shard_map/all_to_all | solution.py:94
  302.7 9.1 %fusion.37 = (f32[1024]{0:T(1024)S(1)}, bf16[1024,1536]{1,0:T(8,128)(2,1)S(1)}) fusion(bf16[1024,1536]{0,1:T(8,128)(2,1)} %bitcast.137, bf16[1536,1536]{1,0:T(8,128)(2,1)} %param.21, bf16[1024,1536]{1,0:T(8,128)(2,1)} %param.15), kind=kOutput, calls=%fused_computation.51 | convolution fusion | flops 4841274368 | bytes 14159872 | tf_op jit(solution)/shard_map/dot_general | solution.py:95
  311.9 35.4 %fusion.43 = f32[1024,8960]{1,0:T(8,128)} fusion(bf16[1536,8960]{1,0:T(8,128)(2,1)} %param.23, bf16[1024,1536]{1,0:T(8,128)(2,1)S(1)} %get-tuple-element.283, f32[1536]{0:T(1024)S(1)} %convert_element_type.58, f32[1024]{0:T(1024)S(1)} %add_rsqrt_fusion), kind=kOutput, calls=%fused_computation.56 | convolution fusion | flops 28192014336 | bytes 67381248 | tf_op jit(solution)/shard_map/dot_general | solution.py:97
  347.2 44.3 %multiply_convert_fusion.clone.6 = bf16[1024,8960]{1,0:T(8,128)(2,1)} fusion(f32[1024,8960]{1,0:T(8,128)} %fusion.43, bf16[1536,8960]{1,0:T(8,128)(2,1)} %param.24, bf16[1024,1536]{1,0:T(8,128)(2,1)S(1)} %get-tuple-element.283, f32[1536]{0:T(1024)S(1)} %convert_element_type.58, f32[1024]{0:T(1024)S(1)} %add_rsqrt_fusion), kind=kOutput, calls=%fused_computation.39.clone.clone.clone.clone.clone.1 | convolution fusion | flops 28247064576 | bytes 85731328 | tf_op jit(solution)/shard_map/dot_general | solution.py:98
  391.6 35.8 %fusion.40 = bf16[1024,1536]{1,0:T(8,128)(2,1)} fusion(bf16[1024,1536]{1,0:T(8,128)(2,1)S(1)} %get-tuple-element.283, bf16[8960,1536]{1,0:T(8,128)(2,1)} %param.25, bf16[1024,8960]{1,0:T(8,128)(2,1)} %multiply_convert_fusion.clone.6), kind=kOutput, calls=%fused_computation.54 | convolution fusion | flops 28190441472 | bytes 52166656 | tf_op jit(solution)/shard_map/dot_general | solution.py:100
  (457 shorter events, 97.4 us)
Async XLA Ops:
  0.6 2.8 copy-start
  0.6 3.1 copy-start.6
  0.7 2.7 copy-start.8
  5.1 6.0 %copy-start.7 = (s32[1024]{0:T(1024)S(1)}, s32[1024]{0:T(1024)}, u32[]{:S(2)}) copy-start(s32[1024]{0:T(1024)} %param.16) | copy-start | bytes 12292
  6.5 18.8 %all-to-all-start.2 = ((bf16[1024,4,128]{2,0,1:T(8,128)(2,1)}), bf16[1024,4,128]{2,0,1:T(8,128)(2,1)S(1)}, u32[]{:S(2)}, u32[]{:S(2)}) async-start(bf16[1024,4,128]{2,0,1:T(8,128)(2,1)} %bitcast.25), calls=%async_computation.2 | async-start | bytes 2097152 | tf_op jit(solution)/shard_map/all_to_all | solution.py:89
  23.7 6.3 %copy-start.10 = (bf16[1536,256]{1,0:T(8,128)(2,1)S(1)}, bf16[1536,256]{1,0:T(8,128)(2,1)}, u32[]{:S(2)}) copy-start(bf16[1536,256]{1,0:T(8,128)(2,1)} %param.19) | copy-start | bytes 2359300
  25.3 62.4 %copy-start.4 = (bf16[1024,4,128]{2,0,1:T(8,128)(2,1)}, bf16[1024,4,128]{2,0,1:T(8,128)(2,1)S(1)}, u32[]{:S(2)}) copy-start(bf16[1024,4,128]{2,0,1:T(8,128)(2,1)S(1)} %all-to-all-done.2) | copy-start | bytes 3145732
  25.3 41.3 %all-to-all-start = ((bf16[1024,12,128]{0,2,1:T(8,128)(2,1)}), bf16[1024,12,128]{0,2,1:T(8,128)(2,1)}, u32[]{:S(2)}, u32[]{:S(2)}) async-start(bf16[1024,12,128]{0,2,1:T(8,128)(2,1)} %pad_maximum_fusion), calls=%async_computation | async-start | bytes 6291456 | tf_op jit(solution)/shard_map/all_to_all | solution.py:87
  67.7 25.2 %all-to-all-start.1 = ((bf16[1024,4,128]{2,0,1:T(8,128)(2,1)}), bf16[1024,4,128]{2,0,1:T(8,128)(2,1)S(1)}, u32[]{:S(2)}, u32[]{:S(2)}) async-start(bf16[1024,4,128]{2,0,1:T(8,128)(2,1)} %bitcast.20), calls=%async_computation.1 | async-start | bytes 2097152 | tf_op jit(solution)/shard_map/all_to_all | solution.py:88
  233.7 7.2 %copy-start.2 = (bf16[4096,1,128]{2,0,1:T(8,128)(2,1)}, bf16[4096,1,128]{2,0,1:T(8,128)(2,1)S(1)}, u32[]{:S(2)}) copy-start(bf16[4096,1,128]{2,0,1:T(8,128)(2,1)S(1)} %get-tuple-element.540) | copy-start | bytes 3145732
  240.9 5.0 %copy-start.9 = (bf16[1536]{0:T(1024)(128)(2,1)S(1)}, bf16[1536]{0:T(1024)(128)(2,1)}, u32[]{:S(2)}) copy-start(bf16[1536]{0:T(1024)(128)(2,1)} %param.22) | copy-start | bytes 9220
  240.9 52.9 %all-to-all-start.3 = ((bf16[4096,3,128]{2,1,0:T(4,128)(2,1)}), bf16[4096,3,128]{2,1,0:T(4,128)(2,1)}, u32[]{:S(2)}, u32[]{:S(2)}) async-start(bf16[4096,3,128]{2,1,0:T(4,128)(2,1)} %copy.49), calls=%async_computation.3 | async-start | bytes 8388608 | tf_op jit(solution)/shard_map/all_to_all | solution.py:94
  391.6 35.8 %copy-start.3 = (bf16[4096,1,128]{2,0,1:T(8,128)(2,1)S(1)}, bf16[4096,1,128]{2,0,1:T(8,128)(2,1)}, u32[]{:S(2)}) copy-start(bf16[4096,1,128]{2,0,1:T(8,128)(2,1)} %copy-done.2) | copy-start | bytes 3145732
  391.6 36.8 %copy-start.5 = (bf16[1024,4,128]{2,0,1:T(8,128)(2,1)S(1)}, bf16[1024,4,128]{2,0,1:T(8,128)(2,1)}, u32[]{:S(2)}) copy-start(bf16[1024,4,128]{2,0,1:T(8,128)(2,1)} %copy-done.4) | copy-start | bytes 3145732
  391.6 37.8 %copy-start.1 = (bf16[1536,256]{1,0:T(8,128)(2,1)S(1)}, bf16[1536,256]{1,0:T(8,128)(2,1)}, u32[]{:S(2)}) copy-start(bf16[1536,256]{1,0:T(8,128)(2,1)} %param.20) | copy-start | bytes 2359300
where the time goes:
time: 430 us; the launch traced here: 429 us
  matrix products  208 us (48%)
  waiting for transfers between devices  82.5 us (19%)
  local copies, waits for them, and re-layouts  52 us (12%)
  other arithmetic  43.1 us (10%)
  starting transfers between devices  17.8 us (4%)
  blocking collectives  16.5 us (4%)
  loops' own time  8.88 us (2%)
    all_to_all x1, waiting for transfers between devices, layer_shard(): lax.all_to_all(attn_heads, 'sp', 0, 1, tiled=True)  47.9 us
    dot_general x36, matrix products, kv_step(): jnp.einsum('qgrk,kgd->qgrd', weights.astype(jnp.bfloat16), v_blk, preferr...  44.9 us
    dot_general x1, matrix products, layer_shard(): up_proj = jnp.dot(g_norm, w_up, preferred_element_type=jnp.float32)  44.3 us
    dot_general x1, matrix products, layer_shard(): jnp.dot(act_mix, w_down, preferred_element_type=jnp.float32)  35.8 us
    dot_general x1, matrix products, layer_shard(): gate_proj = jnp.dot(g_norm, w_gate, preferred_element_type=jnp.float32)  35.4 us
    all_to_all x1, waiting for transfers between devices, layer_shard(): q_heads = lax.all_to_all(q_rot, 'sp', 1, 0, tiled=True)  33 us
    dot_general x36, matrix products, kv_step(): jnp.einsum('qgrd,kgd->qgrk', q_blk, k_blk, preferred_element_type=jnp.flo...  25.3 us
    reduce_sum x36, other arithmetic, kv_step(): run_sum = run_sum * decay_fac + jnp.sum(weights, axis=-1)  25.2 us
  transfers between devices with their start and end apart: 4, of which 3 were waited for; matrix products, arithmetic and copies ran while one was open for 5% of the time, Pallas kernels for 0%

commit v1 on v0

--- a/solution.py
+++ b/solution.py
@@ -1,12 +1,103 @@
+import functools
 import jax
 import jax.numpy as jnp
 from jax import lax
+from jax.experimental import pallas as pl
+from jax.experimental.pallas import tpu as pltpu
+
 from jax.sharding import PartitionSpec as P
 
 HEAD_DIM = 128
 ROPE_THETA = 500000
+BLOCK_LEN = 512
+ROWS = 1024
+DIM = 1536
+FFN = 8960
 NORM_EPS = 1e-5
-BLOCK_LEN = 512
+
+
+def mlp_kernel(fb, rt, o_ref, x_ref, wout_ref, gain_ref, wg_hbm, wu_hbm, wd_hbm, out_ref, acc, g_buf, m_buf, wg, wu, wd, sems):
+    steps = FFN // fb
+
+    def copies(j, slot):
+        off = pl.multiple_of(j * fb, 128)
+        return (
+            pltpu.make_async_copy(wg_hbm.at[:, pl.ds(off, fb)], wg.at[slot], sems.at[slot, 0]),
+            pltpu.make_async_copy(wu_hbm.at[:, pl.ds(off, fb)], wu.at[slot], sems.at[slot, 1]),
+            pltpu.make_async_copy(wd_hbm.at[pl.ds(off, fb), :], wd.at[slot], sems.at[slot, 2]),
+        )
+
+    for c in copies(0, 0):
+        c.start()
+
+    gain = gain_ref[...].astype(jnp.float32)
+
+    def proj(r, _):
+        rows = pl.ds(pl.multiple_of(r * 256, 256), 256)
+        y = x_ref[rows, :].astype(jnp.float32) + jnp.dot(o_ref[rows, :], wout_ref[...], preferred_element_type=jnp.float32)
+        y = y.astype(jnp.bfloat16).astype(jnp.float32)
+        acc[rows, :] = y
+        ms = jnp.mean(y * y, axis=-1, keepdims=True)
+        g_buf[rows, :] = (y * lax.rsqrt(ms + NORM_EPS) * gain).astype(jnp.bfloat16)
+        return 0
+
+    lax.fori_loop(0, ROWS // 256, proj, 0)
+
+    def step(j, _):
+        slot = lax.rem(j, 2)
+        for c in copies(j, slot):
+            c.wait()
+
+        @pl.when(j + 1 < steps)
+        def _():
+            for c in copies(j + 1, 1 - slot):
+                c.start()
+
+        def tile(r, _):
+            rows = pl.ds(pl.multiple_of(r * rt, rt), rt)
+            for c0 in range(0, fb, 256):
+                cols = pl.ds(c0, 256)
+                gate = jnp.dot(g_buf[rows, :], wg[slot, :, cols], preferred_element_type=jnp.float32)
+                up = jnp.dot(g_buf[rows, :], wu[slot, :, cols], preferred_element_type=jnp.float32)
+                m_buf[:, cols] = (gate / (1.0 + jnp.exp(-gate)) * up).astype(jnp.bfloat16)
+            acc[rows, :] += jnp.dot(m_buf[...], wd[slot], preferred_element_type=jnp.float32)
+            return 0
+
+        lax.fori_loop(0, ROWS // rt, tile, 0)
+        return 0
+
+    lax.fori_loop(0, steps, step, 0)
+
+    def fin(r, _):
+        rows = pl.ds(pl.multiple_of(r * 128, 128), 128)
+        out_ref[rows, :] = acc[rows, :].astype(jnp.bfloat16)
+        return 0
+
+    lax.fori_loop(0, ROWS // 128, fin, 0)
+
+
+def mlp_call(o, x, w_out, gain, wg, wu, wd, fb=1280, rt=512):
+    vm = pl.BlockSpec(memory_space=pltpu.VMEM)
+    hbm = pl.BlockSpec(memory_space=pl.ANY)
+    flops = 2 * ROWS * DIM * (DIM + 3 * FFN)
+    return pl.pallas_call(
+        functools.partial(mlp_kernel, fb, rt),
+        out_shape=jax.ShapeDtypeStruct((ROWS, DIM), jnp.bfloat16),
+        in_specs=[vm, vm, vm, vm, hbm, hbm, hbm],
+        out_specs=vm,
+        scratch_shapes=[
+            pltpu.VMEM((ROWS, DIM), jnp.float32),
+            pltpu.VMEM((ROWS, DIM), jnp.bfloat16),
+            pltpu.VMEM((rt, fb), jnp.bfloat16),
+            pltpu.VMEM((2, DIM, fb), jnp.bfloat16),
+            pltpu.VMEM((2, DIM, fb), jnp.bfloat16),
+            pltpu.VMEM((2, fb, DIM), jnp.bfloat16),
+            pltpu.SemaphoreType.DMA((2, 3)),
+        ],
+        compiler_params=pltpu.CompilerParams(vmem_limit_bytes=60 << 20),
+        cost_estimate=pl.CostEstimate(flops=flops, bytes_accessed=3 * DIM * FFN * 2, transcendentals=ROWS * FFN),
+        name="mlp_block",
+    )(o, x, w_out, gain.reshape(1, DIM), wg, wu, wd)
 
 
 def rms_norm(acts_in, gain_vec):
@@ -92,12 +183,7 @@
         q_grp = q_heads.reshape(seq_len, kv_local, heads_local // kv_local, HEAD_DIM)
         attn_heads = causal_attention(q_grp, k_heads, v_heads, pos_all >= 0, 0).reshape(seq_len, heads_local, HEAD_DIM)
         attn_tok = lax.all_to_all(attn_heads, "sp", 0, 1, tiled=True).reshape(tok_rows, heads * HEAD_DIM)
-        x_mid = (hidden.astype(jnp.float32) + jnp.dot(attn_tok, w_out, preferred_element_type=jnp.float32)).astype(jnp.bfloat16)
-        g_norm = rms_norm(x_mid, mlp_gain)
-        gate_proj = jnp.dot(g_norm, w_gate, preferred_element_type=jnp.float32)
-        up_proj = jnp.dot(g_norm, w_up, preferred_element_type=jnp.float32)
-        act_mix = (jax.nn.silu(gate_proj) * up_proj).astype(jnp.bfloat16)
-        hidden_out = (x_mid.astype(jnp.float32) + jnp.dot(act_mix, w_down, preferred_element_type=jnp.float32)).astype(jnp.bfloat16)
+        hidden_out = mlp_call(attn_tok, hidden, w_out, mlp_gain, w_gate, w_up, w_down)
         return hidden_out, k_heads, v_heads
 
     row_spec = P(("dp", "sp"), None)

time: 430 us -> 443 us (1.030)
  Pallas kernels: 0 us -> 101 us
  matrix products: 208 us -> 115 us
  local copies, waits for them, and re-layouts: 52 us -> 56.6 us
    dot_general x4 -> x0, matrix products: 125 us -> none  [the longest x1 44.3 us: layer_shard(): up_proj = jnp.dot(g_norm, w_up, preferred_element_type=jnp.float32)]
    pallas_call x0 -> x1, Pallas kernels: none -> 101 us  [mlp_call(): pl.pallas_call(functools.partial(mlp_kernel, fb, rt), out_shape=jax.Shape...]
    dot_general x36, matrix products: 44.9 us -> 76.7 us  [kv_step(): jnp.einsum('qgrk,kgd->qgrd', weights.astype(jnp.bfloat16), v_blk, preferr...]
    reshape x0 -> x2, local copies, waits for them, and re-layouts: none -> 5.25 us  [the longest x1 4.66 us: layer_shard(): lax.all_to_all(attn_heads, 'sp', 0, 1, tiled=True)]
where the time goes in v1:
time: 443 us; the launch traced here: 441 us
  matrix products  115 us (26%)
  Pallas kernels  101 us (23%)
  waiting for transfers between devices  81.7 us (18%)
  local copies, waits for them, and re-layouts  56.6 us (13%)
  other arithmetic  44.1 us (10%)
  starting transfers between devices  17.8 us (4%)
  blocking collectives  16.5 us (4%)
  loops' own time  8.2 us (2%)
    pallas_call x1, Pallas kernels, mlp_call(): pl.pallas_call(functools.partial(mlp_kernel, fb, rt), out_shape=jax.Shape...  101 us
    dot_general x36, matrix products, kv_step(): jnp.einsum('qgrk,kgd->qgrd', weights.astype(jnp.bfloat16), v_blk, preferr...  76.7 us
    all_to_all x1, waiting for transfers between devices, layer_shard(): lax.all_to_all(attn_heads, 'sp', 0, 1, tiled=True)  47.3 us
    all_to_all x1, waiting for transfers between devices, layer_shard(): q_heads = lax.all_to_all(q_rot, 'sp', 1, 0, tiled=True)  32.8 us
    reduce_sum x36, other arithmetic, kv_step(): run_sum = run_sum * decay_fac + jnp.sum(weights, axis=-1)  25.2 us
    dot_general x36, matrix products, kv_step(): jnp.einsum('qgrd,kgd->qgrk', q_blk, k_blk, preferred_element_type=jnp.flo...  25.1 us
    all_gather x1, blocking collectives, layer_shard(): pos_all = lax.all_gather(positions, 'sp', axis=0, tiled=True)  16.5 us
    all_to_all x2, local copies, waits for them, and re-layouts, layer_shard(): lax.all_to_all(attn_heads, 'sp', 0, 1, tiled=True)  8.96 us
  transfers between devices with their start and end apart: 4, of which 3 were waited for; matrix products, arithmetic and copies ran while one was open for 5% of the time, Pallas kernels for 0%

profile of v1, /device:TPU:0, one launch (start us, length us, event | category | flops | bytes accessed | tf_op | source)
XLA Modules:
  0.0 441.3 jit_solution(10630946440741941975)
XLA Ops:
  1.5 2.9 fusion.32
  7.1 4.6 %all-to-all-start.2 = ((bf16[1024,4,128]{2,0,1:T(8,128)(2,1)}), bf16[1024,4,128]{2,0,1:T(8,128)(2,1)S(1)}, u32[]{:S(2)}, u32[]{:S(2)}) async-start(bf16[1024,4,128]{2,0,1:T(8,128)(2,1)} %bitcast.25), calls=%async_computation.2 | async-start | bytes 2097152 | tf_op jit(solution)/shard_map/all_to_all | solution.py:180
  11.8 8.5 %fusion.38 = f32[1024,1536]{0,1:T(8,128)S(1)} fusion(bf16[1536,1536]{1,0:T(8,128)(2,1)} %param.18, bf16[1024,1536]{1,0:T(8,128)(2,1)} %x_ref.1, f32[1536]{0:T(1024)S(1)} %convert_element_type.32, f32[1024]{0:T(1024)S(1)} %add_rsqrt_fusion), kind=kOutput, calls=%fused_computation.57 | convolution fusion | flops 4838129664 | bytes 14166016 | tf_op jit(solution)/shard_map/dot_general | solution.py:172
  22.4 2.0 pad_maximum_fusion
  24.3 1.6 all-to-all-done.2
  26.0 4.7 %all-to-all-start = ((bf16[1024,12,128]{0,2,1:T(8,128)(2,1)}), bf16[1024,12,128]{0,2,1:T(8,128)(2,1)}, u32[]{:S(2)}, u32[]{:S(2)}) async-start(bf16[1024,12,128]{0,2,1:T(8,128)(2,1)} %pad_maximum_fusion), calls=%async_computation | async-start | bytes 6291456 | tf_op jit(solution)/shard_map/all_to_all | solution.py:178
  30.7 3.3 fusion.36
  34.5 32.8 %all-to-all-done = bf16[1024,12,128]{0,2,1:T(8,128)(2,1)} async-done(((bf16[1024,12,128]{0,2,1:T(8,128)(2,1)}), bf16[1024,12,128]{0,2,1:T(8,128)(2,1)}, u32[]{:S(2)}, u32[]{:S(2)}) %all-to-all-start) | async-done | bytes 3145760 | tf_op jit(solution)/shard_map/all_to_all | solution.py:178
  68.4 3.5 all-to-all-start.1
  71.9 16.5 %all_gather.3 = s32[4096]{0:T(1024)S(1)} all-gather(s32[1024]{0:T(1024)S(1)} %copy-done.5), channel_id=1, replica_groups=mesh['dp'=2,'sp'=4] {'sp'}, dimensions={0}, use_global_device_ids=true | all-gather | bytes 20480 | tf_op jit(solution)/shard_map/all_gather | solution.py:181
  88.4 1.3 copy.38
  89.7 4.6 %copy.34 = bf16[4,1024,3,128]{3,1,0,2:T(8,128)(2,1)} copy(bf16[4,1024,3,128]{1,3,2,0:T(8,128)(2,1)} %bitcast.17) | data formatting | bytes 6291456 | tf_op jit(solution)/shard_map/all_to_all | solution.py:178
  94.4 171.1 %while.43 = (s32[]{:T(128)}, bf16[8,512,1,3,128]{4,1,0,3,2:T(8,128)(2,1)}, s32[8]{0:T(128)S(1)}, bf16[8,512,1,3,128]{4,1,0,3,2:T(8,128)(2,1)}, pred[4096]{0:T(10...) while((s32[]{:T(128)}, ...), condition=%wide.region_6.7_spmd.clone.clone, body=%wide.region_1.6_spmd.clone.clone.sunk | while | flops 412632608 | bytes 17195224 | solution.py:156
  96.7 4.0 while.44
  98.5 2.1 fusion.60
  104.2 8.0 %while.44 = (s32[]{:T(128)}, f32[512,1,3]{0,2,1:T(4,128)S(1)}, f32[512,1,3]{0,2,1:T(4,128)S(1)}, f32[512,1,3,128]{0,3,2,1:T(8,128)S(1)}, s32[]{:T(128)}, /*index...) while((s32[]{:T(128)}, f32[512,1,3]{0,2,1:T(4,128)S(1)}, ...), condition=%wide.region_5.5_spmd, body=%wide.region_2.4_spmd.sunk | while | flops 412235776 | bytes 12834515 | solution.py:153
  106.0 2.1 fusion.60
  110.0 2.1 fusion.60
  115.6 11.9 %while.44 = (s32[]{:T(128)}, f32[512,1,3]{0,2,1:T(4,128)S(1)}, f32[512,1,3]{0,2,1:T(4,128)S(1)}, f32[512,1,3,128]{0,3,2,1:T(8,128)S(1)}, s32[]{:T(128)}, /*index...) while((s32[]{:T(128)}, f32[512,1,3]{0,2,1:T(4,128)S(1)}, ...), condition=%wide.region_5.5_spmd, body=%wide.region_2.4_spmd.sunk | while | flops 412235776 | bytes 12834515 | solution.py:153
  117.5 2.1 fusion.60
  121.4 2.1 fusion.60
  125.4 2.1 fusion.60
  131.1 15.9 %while.44 = (s32[]{:T(128)}, f32[512,1,3]{0,2,1:T(4,128)S(1)}, f32[512,1,3]{0,2,1:T(4,128)S(1)}, f32[512,1,3,128]{0,3,2,1:T(8,128)S(1)}, s32[]{:T(128)}, /*index...) while((s32[]{:T(128)}, f32[512,1,3]{0,2,1:T(4,128)S(1)}, ...), condition=%wide.region_5.5_spmd, body=%wide.region_2.4_spmd.sunk | while | flops 412235776 | bytes 12834515 | solution.py:153
  132.9 2.1 fusion.60
  136.9 2.1 fusion.60
  140.8 2.1 fusion.60
  144.8 2.1 fusion.60
  150.5 19.9 %while.44 = (s32[]{:T(128)}, f32[512,1,3]{0,2,1:T(4,128)S(1)}, f32[512,1,3]{0,2,1:T(4,128)S(1)}, f32[512,1,3,128]{0,3,2,1:T(8,128)S(1)}, s32[]{:T(128)}, /*index...) while((s32[]{:T(128)}, f32[512,1,3]{0,2,1:T(4,128)S(1)}, ...), condition=%wide.region_5.5_spmd, body=%wide.region_2.4_spmd.sunk | while | flops 412235776 | bytes 12834515 | solution.py:153
  152.3 2.1 fusion.60
  156.3 2.1 fusion.60
  160.2 2.1 fusion.60
  164.2 2.1 fusion.60
  168.2 2.1 fusion.60
  173.8 23.9 %while.44 = (s32[]{:T(128)}, f32[512,1,3]{0,2,1:T(4,128)S(1)}, f32[512,1,3]{0,2,1:T(4,128)S(1)}, f32[512,1,3,128]{0,3,2,1:T(8,128)S(1)}, s32[]{:T(128)}, /*index...) while((s32[]{:T(128)}, f32[512,1,3]{0,2,1:T(4,128)S(1)}, ...), condition=%wide.region_5.5_spmd, body=%wide.region_2.4_spmd.sunk | while | flops 412235776 | bytes 12834515 | solution.py:153
  175.7 2.1 fusion.60
  179.7 2.1 fusion.60
  183.6 2.1 fusion.60
  187.6 2.1 fusion.60
  191.6 2.1 fusion.60
  195.6 2.1 fusion.60
  201.2 27.8 %while.44 = (s32[]{:T(128)}, f32[512,1,3]{0,2,1:T(4,128)S(1)}, f32[512,1,3]{0,2,1:T(4,128)S(1)}, f32[512,1,3,128]{0,3,2,1:T(8,128)S(1)}, s32[]{:T(128)}, /*index...) while((s32[]{:T(128)}, f32[512,1,3]{0,2,1:T(4,128)S(1)}, ...), condition=%wide.region_5.5_spmd, body=%wide.region_2.4_spmd.sunk | while | flops 412235776 | bytes 12834515 | solution.py:153
  203.0 2.1 fusion.60
  207.0 2.1 fusion.60
  211.0 2.1 fusion.60
  215.0 2.1 fusion.60
  218.9 2.1 fusion.60
  222.9 2.1 fusion.60
  226.9 2.1 fusion.60
  232.5 31.8 %while.44 = (s32[]{:T(128)}, f32[512,1,3]{0,2,1:T(4,128)S(1)}, f32[512,1,3]{0,2,1:T(4,128)S(1)}, f32[512,1,3,128]{0,3,2,1:T(8,128)S(1)}, s32[]{:T(128)}, /*index...) while((s32[]{:T(128)}, f32[512,1,3]{0,2,1:T(4,128)S(1)}, ...), condition=%wide.region_5.5_spmd, body=%wide.region_2.4_spmd.sunk | while | flops 412235776 | bytes 12834515 | solution.py:153
  234.4 2.1 fusion.60
  238.3 2.1 fusion.60
  242.3 2.1 fusion.60
  246.3 2.1 fusion.60
  250.3 2.1 fusion.60
  254.2 2.1 fusion.60
  258.2 2.1 fusion.60
  262.2 2.1 fusion.60
  265.5 6.8 %copy.40 = bf16[4096,3,128]{2,1,0:T(4,128)(2,1)} copy(bf16[4096,3,128]{2,0,1:T(8,128)(2,1)} %bitcast.128) | data formatting | bytes 6291456 | tf_op jit(solution)/shard_map/reshape;reshape | solution.py:184
  272.3 5.0 %all-to-all-start.3 = ((bf16[4096,3,128]{2,1,0:T(4,128)(2,1)}), bf16[4096,3,128]{2,1,0:T(4,128)(2,1)}, u32[]{:S(2)}, u32[]{:S(2)}) async-start(bf16[4096,3,128]{2,1,0:T(4,128)(2,1)} %copy.40), calls=%async_computation.3 | async-start | bytes 8388608 | tf_op jit(solution)/shard_map/all_to_all | solution.py:185
  277.9 47.3 %all-to-all-done.3 = bf16[4096,3,128]{2,1,0:T(4,128)(2,1)} async-done(((bf16[4096,3,128]{2,1,0:T(4,128)(2,1)}), bf16[4096,3,128]{2,1,0:T(4,128)(2,1)}, u32[]{:S(2)}, u32[]{:S(2)}) %all-to-all-start.3) | async-done | bytes 3145760 | tf_op jit(solution)/shard_map/all_to_all | solution.py:185
  325.1 4.3 copy.41
  329.4 4.7 %copy.42 = bf16[1024,4,3,128]{0,3,2,1:T(8,128)(2,1)} copy(bf16[1024,4,3,128]{3,0,1,2:T(8,128)(2,1)} %bitcast.121) | data formatting | bytes 6291456 | tf_op jit(solution)/shard_map/all_to_all | solution.py:185
  334.1 4.7 %copy.43.o_ref = bf16[1024,1536]{1,0:T(8,128)(2,1)} copy(bf16[1024,1536]{0,1:T(8,128)(2,1)} %bitcast.122) | data formatting | bytes 6291456 | tf_op jit(solution)/shard_map/reshape | solution.py:185
  338.8 100.6 %mlp_block.1 = bf16[1024,1536]{1,0:T(8,128)(2,1)} custom-call(bf16[1024,1536]{1,0:T(8,128)(2,1)} %copy.43.o_ref, bf16[1024,1536]{1,0:T(8,128)(2,1)} %x_ref.1, bf16[1536,1536]{1,0:T(8,128)(2,1)} %wout_ref.1, bf16[1,1536]{1,0:T(2,128)(2,1)} %reshape.179.gain_ref, bf16[1536,8960]{1,0:T(8,128)(2,1)} %wg_hbm.1, bf16[1536,8960]{1,0:T(8,128)(2,1)} %wu_hbm.1, ...), custom_call_target="tpu_custom_call" | custom-call | flops 89389006848 | bytes 82575360 | tf_op jit(solution)/shard_map/mlp_block/pallas_call | solution.py:83
  (446 shorter events, 96.0 us)
Async XLA Ops:
  0.6 3.8 copy-start
  0.6 3.8 copy-start.4
  7.1 18.8 %all-to-all-start.2 = ((bf16[1024,4,128]{2,0,1:T(8,128)(2,1)}), bf16[1024,4,128]{2,0,1:T(8,128)(2,1)S(1)}, u32[]{:S(2)}, u32[]{:S(2)}) async-start(bf16[1024,4,128]{2,0,1:T(8,128)(2,1)} %bitcast.25), calls=%async_computation.2 | async-start | bytes 2097152 | tf_op jit(solution)/shard_map/all_to_all | solution.py:180
  11.8 8.5 %copy-start.5 = (s32[1024]{0:T(1024)S(1)}, s32[1024]{0:T(1024)}, u32[]{:S(2)}) copy-start(s32[1024]{0:T(1024)} %param.16) | copy-start | bytes 12292
  26.0 62.4 %copy-start.2 = (bf16[1024,4,128]{2,0,1:T(8,128)(2,1)}, bf16[1024,4,128]{2,0,1:T(8,128)(2,1)S(1)}, u32[]{:S(2)}) copy-start(bf16[1024,4,128]{2,0,1:T(8,128)(2,1)S(1)} %all-to-all-done.2) | copy-start | bytes 3145732
  26.0 41.3 %all-to-all-start = ((bf16[1024,12,128]{0,2,1:T(8,128)(2,1)}), bf16[1024,12,128]{0,2,1:T(8,128)(2,1)}, u32[]{:S(2)}, u32[]{:S(2)}) async-start(bf16[1024,12,128]{0,2,1:T(8,128)(2,1)} %pad_maximum_fusion), calls=%async_computation | async-start | bytes 6291456 | tf_op jit(solution)/shard_map/all_to_all | solution.py:178
  68.4 26.0 %all-to-all-start.1 = ((bf16[1024,4,128]{2,0,1:T(8,128)(2,1)}), bf16[1024,4,128]{2,0,1:T(8,128)(2,1)S(1)}, u32[]{:S(2)}, u32[]{:S(2)}) async-start(bf16[1024,4,128]{2,0,1:T(8,128)(2,1)} %bitcast.127), calls=%async_computation.1 | async-start | bytes 2097152 | tf_op jit(solution)/shard_map/all_to_all | solution.py:179
  272.3 5.0 %copy-start.6 = (bf16[1536]{0:T(1024)(128)(2,1)S(1)}, bf16[1536]{0:T(1024)(128)(2,1)}, u32[]{:S(2)}) copy-start(bf16[1536]{0:T(1024)(128)(2,1)} %param.22) | copy-start | bytes 9220
  272.3 52.9 %all-to-all-start.3 = ((bf16[4096,3,128]{2,1,0:T(4,128)(2,1)}), bf16[4096,3,128]{2,1,0:T(4,128)(2,1)}, u32[]{:S(2)}, u32[]{:S(2)}) async-start(bf16[4096,3,128]{2,1,0:T(4,128)(2,1)} %copy.40), calls=%async_computation.3 | async-start | bytes 8388608 | tf_op jit(solution)/shard_map/all_to_all | solution.py:185
  338.7 101.6 %copy-start.3 = (bf16[1024,4,128]{2,0,1:T(8,128)(2,1)S(1)}, bf16[1024,4,128]{2,0,1:T(8,128)(2,1)}, u32[]{:S(2)}) copy-start(bf16[1024,4,128]{2,0,1:T(8,128)(2,1)} %copy-done.2) | copy-start | bytes 3145732
  338.7 102.5 %copy-start.1 = (bf16[1536,256]{1,0:T(8,128)(2,1)S(1)}, bf16[1536,256]{1,0:T(8,128)(2,1)}, u32[]{:S(2)}) copy-start(bf16[1536,256]{1,0:T(8,128)(2,1)} %param.20) | copy-start | bytes 2359300

commit v2 on v1

v2 whole, which is shorter than its diff:
```python
import functools
import jax
import jax.numpy as jnp
from jax import lax
from jax.experimental import pallas as pl
from jax.experimental.pallas import tpu as pltpu
from jax.sharding import PartitionSpec as P

ROWS = 1024
DIM = 1536
FFN = 8960
NORM_EPS = 1e-5


def mlp_kernel(fb, rt, o_ref, x_ref, wout_ref, gain_ref, wg_hbm, wu_hbm, wd_hbm, out_ref, acc, g_buf, m_buf, wg, wu, wd, sems):
    steps = FFN // fb

    def copies(j, slot):
        off = pl.multiple_of(j * fb, 128)
        return (
            pltpu.make_async_copy(wg_hbm.at[:, pl.ds(off, fb)], wg.at[slot], sems.at[slot, 0]),
            pltpu.make_async_copy(wu_hbm.at[:, pl.ds(off, fb)], wu.at[slot], sems.at[slot, 1]),
            pltpu.make_async_copy(wd_hbm.at[pl.ds(off, fb), :], wd.at[slot], sems.at[slot, 2]),
        )

    for c in copies(0, 0):
        c.start()

    gain = gain_ref[...].astype(jnp.float32)

    def proj(r, _):
        rows = pl.ds(pl.multiple_of(r * 256, 256), 256)
        y = x_ref[rows, :].astype(jnp.float32) + jnp.dot(o_ref[rows, :], wout_ref[...], preferred_element_type=jnp.float32)
        y = y.astype(jnp.bfloat16).astype(jnp.float32)
        acc[rows, :] = y
        ms = jnp.mean(y * y, axis=-1, keepdims=True)
        g_buf[rows, :] = (y * lax.rsqrt(ms + NORM_EPS) * gain).astype(jnp.bfloat16)
        return 0

    lax.fori_loop(0, ROWS // 256, proj, 0)

    def step(j, _):
        slot = lax.rem(j, 2)
        for c in copies(j, slot):
            c.wait()

        @pl.when(j + 1 < steps)
        def _():
            for c in copies(j + 1, 1 - slot):
                c.start()

        def tile(r, _):
            rows = pl.ds(pl.multiple_of(r * rt, rt), rt)
            for c0 in range(0, fb, 256):
                cols = pl.ds(c0, 256)
                gate = jnp.dot(g_buf[rows, :], wg[slot, :, cols], preferred_element_type=jnp.float32)
                up = jnp.dot(g_buf[rows, :], wu[slot, :, cols], preferred_element_type=jnp.float32)
                m_buf[:, cols] = (gate / (1.0 + jnp.exp(-gate)) * up).astype(jnp.bfloat16)
            acc[rows, :] += jnp.dot(m_buf[...], wd[slot], preferred_element_type=jnp.float32)
            return 0

        lax.fori_loop(0, ROWS // rt, tile, 0)
        return 0

    lax.fori_loop(0, steps, step, 0)

    def fin(r, _):
        rows = pl.ds(pl.multiple_of(r * 128, 128), 128)
        out_ref[rows, :] = acc[rows, :].astype(jnp.bfloat16)
        return 0

    lax.fori_loop(0, ROWS // 128, fin, 0)


def mlp_call(o, x, w_out, gain, wg, wu, wd, fb=1280, rt=512):
    vm = pl.BlockSpec(memory_space=pltpu.VMEM)
    hbm = pl.BlockSpec(memory_space=pl.ANY)
    flops = 2 * ROWS * DIM * (DIM + 3 * FFN)
    return pl.pallas_call(
        functools.partial(mlp_kernel, fb, rt),
        out_shape=jax.ShapeDtypeStruct((ROWS, DIM), jnp.bfloat16),
        in_specs=[vm, vm, vm, vm, hbm, hbm, hbm],
        out_specs=vm,
        scratch_shapes=[
            pltpu.VMEM((ROWS, DIM), jnp.float32),
            pltpu.VMEM((ROWS, DIM), jnp.bfloat16),
            pltpu.VMEM((rt, fb), jnp.bfloat16),
            pltpu.VMEM((2, DIM, fb), jnp.bfloat16),
            pltpu.VMEM((2, DIM, fb), jnp.bfloat16),
            pltpu.VMEM((2, fb, DIM), jnp.bfloat16),
            pltpu.SemaphoreType.DMA((2, 3)),
        ],
        compiler_params=pltpu.CompilerParams(vmem_limit_bytes=60 << 20),
        cost_estimate=pl.CostEstimate(flops=flops, bytes_accessed=3 * DIM * FFN * 2, transcendentals=ROWS * FFN),
        name="mlp_block",
    )(o, x, w_out, gain.reshape(1, DIM), wg, wu, wd)


HEAD_DIM = 128
HEADS = 12
GROUP = 6
ROPE_THETA = 500000
SCALE_LOG2E = 1.4426950408889634 * HEAD_DIM ** -0.5
NEG = -2.0e38
QB = 512
MESH = pl.DeviceIdType.MESH


def attend(q_att, kv, vt, acc, m_s, l_s, tb, src, chunk, kv_head, keys, mask_fn):
    q_src, q_off = tb // 2, pl.multiple_of(lax.rem(tb, 2) * QB, QB)
    k_off = pl.multiple_of(chunk * keys, keys)
    for h in range(GROUP):
        k_blk = kv[src, kv_head, 0, pl.ds(k_off, keys), :]
        q_blk = q_att[q_src, h, pl.ds(q_off, QB), :]
        s = lax.dot_general(k_blk, q_blk, (((1,), (1,)), ((), ())), preferred_element_type=jnp.float32)
        if mask_fn is not None:
            s = mask_fn(s)
        m_prev = m_s[tb, h]
        m_new = jnp.maximum(m_prev, jnp.max(s, axis=0, keepdims=True))
        p = jnp.exp2((s - m_new) * SCALE_LOG2E)
        decay = jnp.exp2((m_prev - m_new) * SCALE_LOG2E)
        l_s[tb, h] = l_s[tb, h] * decay + jnp.sum(p, axis=0, keepdims=True)
        pv = jnp.dot(vt[src, :, pl.ds(k_off, keys)], p.astype(jnp.bfloat16), preferred_element_type=jnp.float32)
        acc[tb, h] = acc[tb, h] * decay + pv
        m_s[tb, h] = m_new


def attn_kernel(pad_ref, x_ref, cos_ref, sin_ref, gain_ref, wq_ref, wk_ref, wv_ref, out_ref, kc_ref, vc_ref,
                h_buf, q_att, q_send, kv, vt, acc, m_s, l_s, o_buf, send_sem, recv_sem, osend_sem, orecv_sem, cache_sem, ocopy_sem):
    me = lax.axis_index("sp")
    x = me // 2
    c = lax.rem(me, 2)
    partner = 2 * x + (1 - c)
    cross = 2 * (1 - x) + c
    diag = 2 * (1 - x) + (1 - c)
    pad = pad_ref[0]

    barrier = pltpu.get_barrier_semaphore()
    for peer in (partner, cross):
        pl.semaphore_signal(barrier, inc=1, device_id={"sp": peer}, device_id_type=MESH)
    pl.semaphore_wait(barrier, 2)

    gain = gain_ref[...].astype(jnp.float32)

    def rope(t, rows):
        return (t * cos_ref[rows, :] + pltpu.roll(t, 64, 1) * sin_ref[rows, :]).astype(jnp.bfloat16)

    def kv_rows(r, _):
        rows = pl.ds(pl.multiple_of(r * 256, 256), 256)
        xf = x_ref[rows, :].astype(jnp.float32)
        ms = jnp.mean(xf * xf, axis=-1, keepdims=True)
        h = (xf * lax.rsqrt(ms + NORM_EPS) * gain).astype(jnp.bfloat16)
        h_buf[rows, :] = h
        k = jnp.dot(h, wk_ref[...], preferred_element_type=jnp.float32)
        v = jnp.dot(h, wv_ref[...], preferred_element_type=jnp.float32).astype(jnp.bfloat16)
        for g in range(2):
            kv[me, g, 0, rows, :] = rope(k[:, g * 128:(g + 1) * 128], rows)
            kv[me, g, 1, rows, :] = v[:, g * 128:(g + 1) * 128]
        return 0

    lax.fori_loop(0, ROWS // 256, kv_rows, 0)

    def kv_copy(src, i, peer):
        return pltpu.make_async_remote_copy(src_ref=kv.at[src], dst_ref=kv.at[src], send_sem=send_sem.at[i], recv_sem=recv_sem.at[i],
                                            device_id={"sp": peer}, device_id_type=MESH)

    to_cross = kv_copy(me, 0, cross)
    to_cross.start()
    to_partner = kv_copy(me, 1, partner)
    to_partner.start()

    def q_rows(dst, head_group):
        def body(r, _):
            rows = pl.ds(pl.multiple_of(r * 256, 256), 256)
            col = pl.multiple_of(head_group * 768, 768)
            q = jnp.dot(h_buf[rows, :], wq_ref[:, pl.ds(col, 768)], preferred_element_type=jnp.float32)
            for h in range(GROUP):
                dst[h, rows, :] = rope(q[:, h * 128:(h + 1) * 128], rows)
            return 0

        lax.fori_loop(0, ROWS // 256, body, 0)

    q_rows(q_send, 1 - c)
    q_copy = pltpu.make_async_remote_copy(src_ref=q_send, dst_ref=q_att.at[c], send_sem=send_sem.at[3], recv_sem=recv_sem.at[3],
                                          device_id={"sp": partner}, device_id_type=MESH)
    q_copy.start()
    q_rows(q_att.at[c], c)

    def flip(src):
        vt[src] = kv[src, c, 1].T

    def cache_copy(src, i):
        rows = pl.ds(pl.multiple_of(src * ROWS, ROWS), ROWS)
        return (pltpu.make_async_copy(kv.at[src, x, 0], kc_ref.at[rows, :], cache_sem.at[i, 0]),
                pltpu.make_async_copy(kv.at[src, x, 1], vc_ref.at[rows, :], cache_sem.at[i, 1]))

    for cp in cache_copy(me, 0):
        cp.start()
    flip(me)
    to_partner.wait_recv()
    for cp in cache_copy(partner, 1):
        cp.start()
    flip(partner)
    q_copy.wait_recv()

    m_s[...] = jnp.full_like(m_s, NEG)
    l_s[...] = jnp.zeros_like(l_s)
    acc[...] = jnp.zeros_like(acc)

    def mask_at(k_base, q_base):
        def mask(s):
            k_idx = lax.broadcasted_iota(jnp.int32, s.shape, 0) + k_base
            q_idx = lax.broadcasted_iota(jnp.int32, s.shape, 1) + q_base
            return jnp.where((k_idx <= q_idx) & (k_idx >= pad), s, NEG)
        return mask

    def local_block(tb, kb, masked):
        base = x * 2 * ROWS
        src = 2 * x + kb // 2
        fn = mask_at(base + kb * QB, base + tb * QB) if masked else None
        attend(q_att, kv, vt, acc, m_s, l_s, tb, src, lax.rem(kb, 2), c, QB, fn)

    def local_tb(tb, _):
        first = jnp.minimum(1 - x, tb)

        def masked(i, _):
            local_block(tb, jnp.where(i == 0, tb, 0), True)
            return 0

        lax.fori_loop(0, 1 + first, masked, 0)

        def plain(kb, _):
            local_block(tb, kb, False)
            return 0

        lax.fori_loop(first, tb, plain, 0)
        return 0

    lax.fori_loop(0, 4, local_tb, 0)

    to_cross.wait_recv()
    forward = kv_copy(cross, 2, partner)
    forward.start()
    for cp in cache_copy(cross, 2):
        cp.start()
    flip(cross)
    kv_copy(diag, 2, partner).wait_recv()
    for cp in cache_copy(diag, 3):
        cp.start()
    flip(diag)

    def o_copies(i, tb):
        rows = pl.ds(pl.multiple_of(lax.rem(tb, 2) * QB, QB), QB)
        cols = pl.ds(pl.multiple_of(c * 768, 768), 768)
        return pltpu.make_async_remote_copy(src_ref=o_buf.at[tb], dst_ref=out_ref.at[rows, cols], send_sem=osend_sem.at[i], recv_sem=orecv_sem.at[i],
                                            device_id={"sp": partner}, device_id_type=MESH), pltpu.make_async_copy(o_buf.at[tb], out_ref.at[rows, cols], ocopy_sem.at[i])

    def finish(tb):
        def remote(src, _):
            def pad_mask(s):
                k_idx = lax.broadcasted_iota(jnp.int32, s.shape, 0) + src * ROWS
                return jnp.where(k_idx >= pad, s, NEG)

            attend(q_att, kv, vt, acc, m_s, l_s, tb, src, 0, c, ROWS, pad_mask)
            return 0

        lax.fori_loop(0, 2 * x, remote, 0)
        q_idx = lax.broadcasted_iota(jnp.int32, (1, QB), 1) + (x * 2 * ROWS + tb * QB)
        for h in range(GROUP):
            inv = jnp.where(q_idx >= pad, 1.0 / l_s[tb, h], 0.0)
            o_buf[tb, :, h * 128:(h + 1) * 128] = (acc[tb, h] * inv).T.astype(jnp.bfloat16)

    def partner_tb(i, _):
        tb = 2 * (1 - c) + i
        finish(tb)
        o_copies(i, tb)[0].start()
        return 0

    lax.fori_loop(0, 2, partner_tb, 0)

    def own_tb(i, _):
        tb = 2 * c + i
        finish(tb)
        o_copies(i, tb)[1].start()
        return 0

    lax.fori_loop(0, 2, own_tb, 0)

    to_cross.wait_send()
    to_partner.wait_send()
    forward.wait_send()
    q_copy.wait_send()
    for i, src in enumerate((me, partner, cross, diag)):
        for cp in cache_copy(src, i):
            cp.wait()
    for i in range(2):
        o_copies(i, 2 * (1 - c) + i)[0].wait_send()
        o_copies(i, 2 * c + i)[1].wait()
    for i in range(2):
        rows = pl.ds(i * QB, QB)
        cols = pl.ds(pl.multiple_of((1 - c) * 768, 768), 768)
        pltpu.make_async_remote_copy(src_ref=o_buf.at[i], dst_ref=out_ref.at[rows, cols], send_sem=osend_sem.at[i], recv_sem=orecv_sem.at[i],
                                     device_id={"sp": partner}, device_id_type=MESH).wait_recv()


def attn_call(pad, x, cos, sin, gain, w_query, w_key, w_value):
    vm = pl.BlockSpec(memory_space=pltpu.VMEM)
    hbm = pl.BlockSpec(memory_space=pl.ANY)
    flops = 2 * ROWS * DIM * 2048 + 4 * 128 * 3 * 4096 * 2048
    bf = jnp.bfloat16
    return pl.pallas_call(
        attn_kernel,
        out_shape=(jax.ShapeDtypeStruct((ROWS, DIM), bf), jax.ShapeDtypeStruct((4 * ROWS, 128), bf), jax.ShapeDtypeStruct((4 * ROWS, 128), bf)),
        in_specs=[pl.BlockSpec(memory_space=pltpu.SMEM)] + [vm] * 7,
        out_specs=(hbm, hbm, hbm),
        scratch_shapes=[
            pltpu.VMEM((ROWS, DIM), bf),
            pltpu.VMEM((2, GROUP, ROWS, 128), bf),
            pltpu.VMEM((GROUP, ROWS, 128), bf),
            pltpu.VMEM((4, 2, 2, ROWS, 128), bf),
            pltpu.VMEM((4, 128, ROWS), bf),
            pltpu.VMEM((4, GROUP, 128, QB), jnp.float32),
            pltpu.VMEM((4, GROUP, 1, QB), jnp.float32),
            pltpu.VMEM((4, GROUP, 1, QB), jnp.float32),
            pltpu.VMEM((4, QB, 768), bf),
            pltpu.SemaphoreType.DMA((4,)),
            pltpu.SemaphoreType.DMA((4,)),
            pltpu.SemaphoreType.DMA((2,)),
            pltpu.SemaphoreType.DMA((2,)),
            pltpu.SemaphoreType.DMA((4, 2)),
            pltpu.SemaphoreType.DMA((2,)),
        ],
        compiler_params=pltpu.CompilerParams(vmem_limit_bytes=60 << 20, collective_id=0, has_side_effects=True),
        cost_estimate=pl.CostEstimate(flops=flops, bytes_accessed=20 << 20, transcendentals=3 * 4096 * 2048),
        name="attn_block",
    )(pad, x, cos, sin, gain.reshape(1, DIM), w_query, w_key, w_value)


def solution(mesh):
    def layer_shard(hidden, positions, attn_gain, w_query, w_key, w_value, w_out, mlp_gain, w_gate, w_up, w_down):
        inv_freq = 1.0 / (ROPE_THETA ** (jnp.arange(0, HEAD_DIM, 2, dtype=jnp.float32) / HEAD_DIM))
        angles = positions.astype(jnp.float32)[:, None] * inv_freq[None, :]
        cos, sin = jnp.cos(angles), jnp.sin(angles)
        cos = jnp.concatenate([cos, cos], axis=-1)
        sin = jnp.concatenate([-sin, sin], axis=-1)
        pad = (lax.axis_index("sp") * ROWS + ROWS - 1 - positions[ROWS - 1]).reshape(1)
        attn, k_cache, v_cache = attn_call(pad, hidden, cos, sin, attn_gain, w_query, w_key, w_value)
        hidden_out = mlp_call(attn, hidden, w_out, mlp_gain, w_gate, w_up, w_down)
        return hidden_out, k_cache.reshape(4 * ROWS, 1, 128), v_cache.reshape(4 * ROWS, 1, 128)

    row_spec = P(("dp", "sp"), None)
    cache_spec = P("dp", "sp", None)
    return jax.shard_map(layer_shard, mesh=mesh, in_specs=(row_spec, P(("dp", "sp")), P(), P(), P(), P(), P(), P(), P(), P(), P()), out_specs=(row_spec, cache_spec, cache_spec), check_vma=False)
```

time: 443 us -> 215 us (0.49)
  the two profiles are of different devices: /device:TPU:0 before, /device:TPU:7 now
where the time goes in v2:
time: 215 us; the launch traced here: 214 us
  Pallas kernels  203 us (94%)
  local copies, waits for them, and re-layouts  5.79 us (3%)
  other arithmetic  3.91 us (2%)
    pallas_call x1, Pallas kernels, attn_call(): pl.pallas_call(attn_kernel, out_shape=(jax.ShapeDtypeStruct((ROWS, DIM),...  103 us
    pallas_call x1, Pallas kernels, mlp_call(): pl.pallas_call(functools.partial(mlp_kernel, fb, rt), out_shape=jax.Shape...  101 us

profile of v2, /device:TPU:7, one launch (start us, length us, event | category | flops | bytes accessed | tf_op | source)
XLA Modules:
  0.0 214.5 jit_solution(14960658267845368050)
XLA Ops:
  0.6 1.3 slice.3
  2.6 0.7 convert_element_type.3
  3.3 1.3 reshape.29.gain_ref
  4.5 1.3 reshape.30.gain_ref
  5.8 1.9 fusion
  7.7 1.3 pad_maximum_fusion
  9.0 102.8 %attn_block.1 = (bf16[1024,1536]{1,0:T(8,128)(2,1)}, bf16[4096,128]{1,0:T(8,128)(2,1)}, bf16[4096,128]{1,0:T(8,128)(2,1)}) custom-call(s32[1]{0:T(128)} %bitcast.1.pad_ref, bf16[1024,1536]{1,0:T(8,128)(2,1)} %x_ref.3, f32[1024,128]{1,0:T(8,128)} %get-tuple-element.12.cos_ref, f32[1024,128]{1,0:T(8,128)} %get-tuple-element.13.sin_ref, ...), custom_call_target="tpu_custom_call" | custom-call | flops 19327352832 | bytes 20971520 | tf_op jit(solution)/shard_map/attn_block/pallas_call | solution.py:311
  111.9 0.0 copy-start.1
  111.9 0.0 copy-start
  111.9 100.6 %mlp_block.1 = bf16[1024,1536]{1,0:T(8,128)(2,1)} custom-call(bf16[1024,1536]{1,0:T(8,128)(2,1)} %get-tuple-element.6.o_ref, bf16[1024,1536]{1,0:T(8,128)(2,1)} %x_ref.3, bf16[1536,1536]{1,0:T(8,128)(2,1)} %wout_ref.1, bf16[1,1536]{1,0:T(2,128)(2,1)} %reshape.30.gain_ref, bf16[1536,8960]{1,0:T(8,128)(2,1)} %wg_hbm.1, bf16[1536,8960]{1,0:T(8,128)(2,1)} %wu_hbm.1, ...), custom_call_target="tpu_custom_call" | custom-call | flops 89389006848 | bytes 82575360 | tf_op jit(solution)/shard_map/mlp_block/pallas_call | solution.py:79
  212.5 0.0 copy-done.1
  212.5 1.0 copy.16
  213.5 0.0 copy-done
  213.5 1.0 copy.17
  (1 shorter events, 0.0 us)
Async XLA Ops:
  111.9 100.6 %copy-start.1 = (bf16[4096,128]{1,0:T(8,128)(2,1)S(1)}, bf16[4096,128]{1,0:T(8,128)(2,1)}, u32[]{:S(2)}) copy-start(bf16[4096,128]{1,0:T(8,128)(2,1)} %get-tuple-element.7) | copy-start | bytes 3145732
  111.9 101.6 %copy-start = (bf16[4096,128]{1,0:T(8,128)(2,1)S(1)}, bf16[4096,128]{1,0:T(8,128)(2,1)}, u32[]{:S(2)}) copy-start(bf16[4096,128]{1,0:T(8,128)(2,1)} %get-tuple-element.8) | copy-start | bytes 3145732

commit v3 on v2

--- a/solution.py
+++ b/solution.py
@@ -1,4 +1,5 @@
 import functools
+import itertools
 import jax
 import jax.numpy as jnp
 from jax import lax
@@ -103,30 +104,82 @@
 SCALE_LOG2E = 1.4426950408889634 * HEAD_DIM ** -0.5
 NEG = -2.0e38
 QB = 512
+KC = 256
+PC = 64
 MESH = pl.DeviceIdType.MESH
 
 
-def attend(q_att, kv, vt, acc, m_s, l_s, tb, src, chunk, kv_head, keys, mask_fn):
-    q_src, q_off = tb // 2, pl.multiple_of(lax.rem(tb, 2) * QB, QB)
-    k_off = pl.multiple_of(chunk * keys, keys)
-    for h in range(GROUP):
-        k_blk = kv[src, kv_head, 0, pl.ds(k_off, keys), :]
-        q_blk = q_att[q_src, h, pl.ds(q_off, QB), :]
-        s = lax.dot_general(k_blk, q_blk, (((1,), (1,)), ((), ())), preferred_element_type=jnp.float32)
-        if mask_fn is not None:
-            s = mask_fn(s)
-        m_prev = m_s[tb, h]
-        m_new = jnp.maximum(m_prev, jnp.max(s, axis=0, keepdims=True))
-        p = jnp.exp2((s - m_new) * SCALE_LOG2E)
-        decay = jnp.exp2((m_prev - m_new) * SCALE_LOG2E)
-        l_s[tb, h] = l_s[tb, h] * decay + jnp.sum(p, axis=0, keepdims=True)
-        pv = jnp.dot(vt[src, :, pl.ds(k_off, keys)], p.astype(jnp.bfloat16), preferred_element_type=jnp.float32)
-        acc[tb, h] = acc[tb, h] * decay + pv
-        m_s[tb, h] = m_new
+def flash_run(n, item_fn, head_sel, biased, q_att, kv, vt, acc, m_s, l_s, s_buf, p_buf, top_s, decay_s, bias):
+    def scores(i, pair):
+        tb, src, chunk, b = item_fn(i)
+        q_off = pl.multiple_of(lax.rem(tb, 2) * QB, QB)
+        k_off = pl.multiple_of(chunk * QB, QB)
+        for u in range(2):
+            q_blk = q_att[tb // 2, 2 * pair + u, pl.ds(q_off, QB), :]
+            top = jnp.full((8, QB), NEG, jnp.float32)
+            for k0 in range(0, QB, KC):
+                k_blk = kv[src, head_sel, 0, pl.ds(k_off + k0, KC), :]
+                s = lax.dot_general(k_blk, q_blk, (((1,), (1,)), ((), ())), preferred_element_type=jnp.float32)
+                if biased:
+                    s = s + bias[b, k0:k0 + KC, :]
+                s_buf[pair, u, k0:k0 + KC, :] = s
+                top = jnp.maximum(top, jnp.max(s.reshape(KC // 8, 8, QB), axis=0))
+                yield
+            top_s[pair, u] = top
+
+    def weights(i, pair):
+        tb = item_fn(i)[0]
+        for u in range(2):
+            h = 2 * pair + u
+            m_prev = m_s[tb, h]
+            m_new = jnp.maximum(m_prev, jnp.max(top_s[pair, u], axis=0, keepdims=True))
+            m8 = jnp.broadcast_to(m_new, (8, QB))
+            total = jnp.zeros((8, QB), jnp.float32)
+            for k0 in range(0, QB, PC):
+                s = s_buf[pair, u, k0:k0 + PC, :].reshape(PC // 8, 8, QB)
+                p = jnp.exp2((s - m8[None]) * SCALE_LOG2E)
+                total = total + jnp.sum(p, axis=0)
+                p_buf[pair, u, k0:k0 + PC, :] = p.reshape(PC, QB).astype(jnp.bfloat16)
+                if (k0 + PC) % KC == 0:
+                    yield
+            decay = jnp.exp2((m_prev - m_new) * SCALE_LOG2E)
+            decay_s[pair, u] = decay
+            l_s[tb, h] = l_s[tb, h] * decay + jnp.sum(total, axis=0, keepdims=True)
+            m_s[tb, h] = m_new
+
+    def values(i, pair):
+        tb, src, chunk, _ = item_fn(i)
+        k_off = pl.multiple_of(chunk * QB, QB)
+        for u in range(2):
+            h = 2 * pair + u
+            pv = jnp.dot(vt[src, :, pl.ds(k_off, QB)], p_buf[pair, u], preferred_element_type=jnp.float32)
+            acc[tb, h] = acc[tb, h] * decay_s[pair, u] + pv
+            for _ in range(QB // KC):
+                yield
+
+    def together(*parts):
+        for _ in itertools.zip_longest(*parts):
+            pass
+
+    @pl.when(n > 0)
+    def _():
+        p_buf[2] = jnp.zeros_like(p_buf[2])
+        decay_s[2] = jnp.ones_like(decay_s[2])
+        together(scores(0, 0))
+
+        def step(i, _):
+            nxt = jnp.minimum(i + 1, n - 1)
+            together(weights(i, 0), scores(i, 1), values(jnp.maximum(i - 1, 0), 2))
+            together(weights(i, 1), scores(i, 2), values(i, 0))
+            together(weights(i, 2), scores(nxt, 0), values(i, 1))
+            return 0
+
+        lax.fori_loop(0, n, step, 0)
+        together(values(n - 1, 2))
 
 
 def attn_kernel(pad_ref, x_ref, cos_ref, sin_ref, gain_ref, wq_ref, wk_ref, wv_ref, out_ref, kc_ref, vc_ref,
-                h_buf, q_att, q_send, kv, vt, acc, m_s, l_s, o_buf, send_sem, recv_sem, osend_sem, orecv_sem, cache_sem, ocopy_sem):
+                h_buf, q_att, q_send, kv, vt, acc, m_s, l_s, s_buf, p_buf, top_s, decay_s, bias, o_buf, send_sem, recv_sem, osend_sem, orecv_sem, cache_sem, ocopy_sem):
     me = lax.axis_index("sp")
     x = me // 2
     c = lax.rem(me, 2)
@@ -207,36 +260,28 @@
     l_s[...] = jnp.zeros_like(l_s)
     acc[...] = jnp.zeros_like(acc)
 
-    def mask_at(k_base, q_base):
-        def mask(s):
-            k_idx = lax.broadcasted_iota(jnp.int32, s.shape, 0) + k_base
-            q_idx = lax.broadcasted_iota(jnp.int32, s.shape, 1) + q_base
-            return jnp.where((k_idx <= q_idx) & (k_idx >= pad), s, NEG)
-        return mask
-
-    def local_block(tb, kb, masked):
-        base = x * 2 * ROWS
-        src = 2 * x + kb // 2
-        fn = mask_at(base + kb * QB, base + tb * QB) if masked else None
-        attend(q_att, kv, vt, acc, m_s, l_s, tb, src, lax.rem(kb, 2), c, QB, fn)
-
-    def local_tb(tb, _):
-        first = jnp.minimum(1 - x, tb)
-
-        def masked(i, _):
-            local_block(tb, jnp.where(i == 0, tb, 0), True)
-            return 0
-
-        lax.fori_loop(0, 1 + first, masked, 0)
-
-        def plain(kb, _):
-            local_block(tb, kb, False)
-            return 0
-
-        lax.fori_loop(first, tb, plain, 0)
-        return 0
-
-    lax.fori_loop(0, 4, local_tb, 0)
+    tri = lax.broadcasted_iota(jnp.int32, (QB, QB), 0) <= lax.broadcasted_iota(jnp.int32, (QB, QB), 1)
+    real = lax.broadcasted_iota(jnp.int32, (QB, QB), 0) >= pad
+    bias[0] = jnp.where(tri, 0.0, NEG)
+    bias[1] = jnp.where(real, 0.0, NEG)
+    bias[2] = jnp.where(tri & real, 0.0, NEG)
+
+    def flash(n, item_fn, biased):
+        flash_run(n, item_fn, c, biased, q_att, kv, vt, acc, m_s, l_s, s_buf, p_buf, top_s, decay_s, bias)
+
+    def local_masked(i):
+        tb = jnp.where(i < 4, i, i - 3)
+        kb = jnp.where(i < 4, i, 0)
+        b = jnp.where(i < 4, jnp.where((i == 0) & (x == 0), 2, 0), 1)
+        return tb, 2 * x + kb // 2, lax.rem(kb, 2), b
+
+    def local_plain(i):
+        tb = jnp.where(x == 0, 2 + jnp.minimum(i, 1), 1 + jnp.minimum(i, 1) + jnp.where(i >= 3, 1, 0))
+        kb = jnp.where(x == 0, 1 + i // 2, i - (tb * (tb - 1)) // 2)
+        return tb, 2 * x + kb // 2, lax.rem(kb, 2), 0
+
+    flash(4 + 3 * (1 - x), local_masked, True)
+    flash(3 + 3 * x, local_plain, False)
 
     to_cross.wait_recv()
     forward = kv_copy(cross, 2, partner)
@@ -255,16 +300,17 @@
         return pltpu.make_async_remote_copy(src_ref=o_buf.at[tb], dst_ref=out_ref.at[rows, cols], send_sem=osend_sem.at[i], recv_sem=orecv_sem.at[i],
                                             device_id={"sp": partner}, device_id_type=MESH), pltpu.make_async_copy(o_buf.at[tb], out_ref.at[rows, cols], ocopy_sem.at[i])
 
+    def remote_masked(i):
+        return i, 0, 0, 1
+
+    def remote_plain(i):
+        kb = 1 + lax.rem(i, 3)
+        return i // 3, kb // 2, lax.rem(kb, 2), 0
+
+    flash(4 * x, remote_masked, True)
+    flash(12 * x, remote_plain, False)
+
     def finish(tb):
-        def remote(src, _):
-            def pad_mask(s):
-                k_idx = lax.broadcasted_iota(jnp.int32, s.shape, 0) + src * ROWS
-                return jnp.where(k_idx >= pad, s, NEG)
-
-            attend(q_att, kv, vt, acc, m_s, l_s, tb, src, 0, c, ROWS, pad_mask)
-            return 0
-
-        lax.fori_loop(0, 2 * x, remote, 0)
         q_idx = lax.broadcasted_iota(jnp.int32, (1, QB), 1) + (x * 2 * ROWS + tb * QB)
         for h in range(GROUP):
             inv = jnp.where(q_idx >= pad, 1.0 / l_s[tb, h], 0.0)
@@ -322,6 +368,11 @@
             pltpu.VMEM((4, GROUP, 128, QB), jnp.float32),
             pltpu.VMEM((4, GROUP, 1, QB), jnp.float32),
             pltpu.VMEM((4, GROUP, 1, QB), jnp.float32),
+            pltpu.VMEM((3, 2, QB, QB), jnp.float32),
+            pltpu.VMEM((3, 2, QB, QB), bf),
+            pltpu.VMEM((3, 2, 8, QB), jnp.float32),
+            pltpu.VMEM((3, 2, 1, QB), jnp.float32),
+            pltpu.VMEM((3, QB, QB), jnp.float32),
             pltpu.VMEM((4, QB, 768), bf),
             pltpu.SemaphoreType.DMA((4,)),
             pltpu.SemaphoreType.DMA((4,)),

time: 215 us -> 197 us (0.916)
  Pallas kernels: 203 us -> 186 us
    pallas_call x1, Pallas kernels: 103 us -> 85.1 us  [attn_call(): pl.pallas_call(attn_kernel, out_shape=(jax.ShapeDtypeStruct((ROWS, DIM),...]
where the time goes in v3:
time: 197 us
  Pallas kernels  186 us (94%)
  local copies, waits for them, and re-layouts  5.79 us (3%)
  other arithmetic  3.91 us (2%)
    pallas_call x1, Pallas kernels, mlp_call(): pl.pallas_call(functools.partial(mlp_kernel, fb, rt), out_shape=jax.Shape...  101 us
    pallas_call x1, Pallas kernels, attn_call(): pl.pallas_call(attn_kernel, out_shape=(jax.ShapeDtypeStruct((ROWS, DIM),...  85.1 us

profile of v3, /device:TPU:7, one launch (start us, length us, event | category | flops | bytes accessed | tf_op | source)
XLA Modules:
  0.0 196.7 jit_solution(18424874184369859601)
XLA Ops:
  0.6 1.3 slice.3
  2.6 0.7 convert_element_type.3
  3.3 1.3 reshape.29.gain_ref
  4.5 1.3 reshape.30.gain_ref
  5.8 1.9 fusion
  7.7 1.3 pad_maximum_fusion
  9.0 85.1 %attn_block.1 = (bf16[1024,1536]{1,0:T(8,128)(2,1)}, bf16[4096,128]{1,0:T(8,128)(2,1)}, bf16[4096,128]{1,0:T(8,128)(2,1)}) custom-call(s32[1]{0:T(128)} %bitcast.1.pad_ref, bf16[1024,1536]{1,0:T(8,128)(2,1)} %x_ref.3, f32[1024,128]{1,0:T(8,128)} %get-tuple-element.12.cos_ref, f32[1024,128]{1,0:T(8,128)} %get-tuple-element.13.sin_ref, ...), custom_call_target="tpu_custom_call" | custom-call | flops 19327352832 | bytes 20971520 | tf_op jit(solution)/shard_map/attn_block/pallas_call | solution.py:357
  94.1 0.0 copy-start.1
  94.1 0.0 copy-start
  94.1 100.6 %mlp_block.1 = bf16[1024,1536]{1,0:T(8,128)(2,1)} custom-call(bf16[1024,1536]{1,0:T(8,128)(2,1)} %get-tuple-element.6.o_ref, bf16[1024,1536]{1,0:T(8,128)(2,1)} %x_ref.3, bf16[1536,1536]{1,0:T(8,128)(2,1)} %wout_ref.1, bf16[1,1536]{1,0:T(2,128)(2,1)} %reshape.30.gain_ref, bf16[1536,8960]{1,0:T(8,128)(2,1)} %wg_hbm.1, bf16[1536,8960]{1,0:T(8,128)(2,1)} %wu_hbm.1, ...), custom_call_target="tpu_custom_call" | custom-call | flops 89389006848 | bytes 82575360 | tf_op jit(solution)/shard_map/mlp_block/pallas_call | solution.py:80
  194.8 0.0 copy-done.1
  194.8 1.0 copy.16
  195.7 0.0 copy-done
  195.7 1.0 copy.17
  (1 shorter events, 0.0 us)
Async XLA Ops:
  94.1 100.6 %copy-start.1 = (bf16[4096,128]{1,0:T(8,128)(2,1)S(1)}, bf16[4096,128]{1,0:T(8,128)(2,1)}, u32[]{:S(2)}) copy-start(bf16[4096,128]{1,0:T(8,128)(2,1)} %get-tuple-element.7) | copy-start | bytes 3145732
  94.1 101.6 %copy-start = (bf16[4096,128]{1,0:T(8,128)(2,1)S(1)}, bf16[4096,128]{1,0:T(8,128)(2,1)}, u32[]{:S(2)}) copy-start(bf16[4096,128]{1,0:T(8,128)(2,1)} %get-tuple-element.8) | copy-start | bytes 3145732

commit v4 on v3

v4 whole, which is shorter than its diff:
```python
import functools
import itertools
import jax
import jax.numpy as jnp
import numpy as np
from jax import lax
from jax.experimental import pallas as pl
from jax.experimental.pallas import tpu as pltpu
from jax.sharding import PartitionSpec as P

ROWS = 1024
DIM = 1536
FFN = 8960
NORM_EPS = 1e-5


def mlp_kernel(fb, rt, o_ref, x_ref, wout_ref, gain_ref, wg_hbm, wu_hbm, wd_hbm, k_in, v_in, out_ref, k_out, v_out, acc, g_buf, m_buf, wg, wu, wd, c_buf, sems, c_sems):
    steps = FFN // fb

    def copies(j, slot):
        off = pl.multiple_of(j * fb, 128)
        return (
            pltpu.make_async_copy(wg_hbm.at[:, pl.ds(off, fb)], wg.at[slot], sems.at[slot, 0]),
            pltpu.make_async_copy(wu_hbm.at[:, pl.ds(off, fb)], wu.at[slot], sems.at[slot, 1]),
            pltpu.make_async_copy(wd_hbm.at[pl.ds(off, fb), :], wd.at[slot], sems.at[slot, 2]),
        )

    for c in copies(0, 0):
        c.start()

    cache = ((k_in, k_out), (v_in, v_out))
    for i in range(2):
        pltpu.make_async_copy(cache[i][0], c_buf.at[i], c_sems.at[0, i]).start()
    gain = gain_ref[...].reshape(1, DIM).astype(jnp.float32)

    def proj(r, _):
        rows = pl.ds(pl.multiple_of(r * 256, 256), 256)
        y = x_ref[rows, :].astype(jnp.float32) + jnp.dot(o_ref[rows, :], wout_ref[...], preferred_element_type=jnp.float32)
        y = y.astype(jnp.bfloat16).astype(jnp.float32)
        acc[rows, :] = y
        ms = jnp.mean(y * y, axis=-1, keepdims=True)
        g_buf[rows, :] = (y * lax.rsqrt(ms + NORM_EPS) * gain).astype(jnp.bfloat16)
        return 0

    lax.fori_loop(0, ROWS // 256, proj, 0)
    for i in range(2):
        pltpu.make_async_copy(cache[i][0], c_buf.at[i], c_sems.at[0, i]).wait()
        pltpu.make_async_copy(c_buf.at[i], cache[i][1], c_sems.at[1, i]).start()

    def step(j, _):
        slot = lax.rem(j, 2)
        for c in copies(j, slot):
            c.wait()

        @pl.when(j + 1 < steps)
        def _():
            for c in copies(j + 1, 1 - slot):
                c.start()

        def tile(r, _):
            rows = pl.ds(pl.multiple_of(r * rt, rt), rt)
            for c0 in range(0, fb, 256):
                cols = pl.ds(c0, 256)
                gate = jnp.dot(g_buf[rows, :], wg[slot, :, cols], preferred_element_type=jnp.float32)
                up = jnp.dot(g_buf[rows, :], wu[slot, :, cols], preferred_element_type=jnp.float32)
                m_buf[:, cols] = (gate / (1.0 + jnp.exp(-gate)) * up).astype(jnp.bfloat16)
            acc[rows, :] += jnp.dot(m_buf[...], wd[slot], preferred_element_type=jnp.float32)
            return 0

        lax.fori_loop(0, ROWS // rt, tile, 0)
        return 0

    lax.fori_loop(0, steps, step, 0)

    def fin(r, _):
        rows = pl.ds(pl.multiple_of(r * 128, 128), 128)
        out_ref[rows, :] = acc[rows, :].astype(jnp.bfloat16)
        return 0

    lax.fori_loop(0, ROWS // 128, fin, 0)
    for i in range(2):
        pltpu.make_async_copy(c_buf.at[i], cache[i][1], c_sems.at[1, i]).wait()


def mlp_call(o, x, w_out, gain, wg, wu, wd, k_all, v_all, fb=1280, rt=512):
    vm = pl.BlockSpec(memory_space=pltpu.VMEM)
    hbm = pl.BlockSpec(memory_space=pl.ANY)
    flops = 2 * ROWS * DIM * (DIM + 3 * FFN)
    return pl.pallas_call(
        functools.partial(mlp_kernel, fb, rt),
        out_shape=(jax.ShapeDtypeStruct((ROWS, DIM), jnp.bfloat16),) + (jax.ShapeDtypeStruct(k_all.shape, jnp.bfloat16),) * 2,
        in_specs=[vm] * 4 + [hbm] * 5,
        out_specs=(vm, hbm, hbm),
        scratch_shapes=[
            pltpu.VMEM((ROWS, DIM), jnp.float32),
            pltpu.VMEM((ROWS, DIM), jnp.bfloat16),
            pltpu.VMEM((rt, fb), jnp.bfloat16),
            pltpu.VMEM((2, DIM, fb), jnp.bfloat16),
            pltpu.VMEM((2, DIM, fb), jnp.bfloat16),
            pltpu.VMEM((2, fb, DIM), jnp.bfloat16),
            pltpu.VMEM((2, 4 * ROWS, 128), jnp.bfloat16),
            pltpu.SemaphoreType.DMA((2, 3)),
            pltpu.SemaphoreType.DMA((2, 2)),
        ],
        compiler_params=pltpu.CompilerParams(vmem_limit_bytes=60 << 20),
        cost_estimate=pl.CostEstimate(flops=flops, bytes_accessed=3 * DIM * FFN * 2, transcendentals=ROWS * FFN),
        name="mlp_block",
    )(o, x, w_out, gain, wg, wu, wd, k_all, v_all)


HEAD_DIM = 128
ROPE_THETA = 500000
SCALE_LOG2E = 1.4426950408889634 * HEAD_DIM ** -0.5
NEG = -2.0e38
QB = 512
KC = 256
PC = 64
FOREIGN = 3
TRI, REAL, BOTH, NONE, FREE = range(5)
MESH = pl.DeviceIdType.MESH


def schedules():
    def code(st, kb, b):
        return (st * 8 + kb) * 8 + b

    a_masked = [code(3 * tb + p, tb, BOTH if tb == 0 else TRI) for tb in range(4) for p in range(3)]
    a_masked += [code(3 * tb + p, 0, REAL) for tb in range(1, 4) for p in range(3)]
    a_plain = [code(3 * tb + p, kb, FREE) for tb in range(2, 4) for kb in range(1, tb) for p in range(3)]
    a_masked.append(a_plain.pop(0))
    a_masked += [a_plain[-1] - FREE + NONE] * 2
    pairs = {tb: 2 if tb < FOREIGN else 3 for tb in range(4)}
    b_masked = [code(3 * tb + p, 4 + tb, TRI) for tb in range(4) for p in range(pairs[tb])]
    b_plain = [code(3 * tb + p, 4 + kb, FREE) for tb in range(1, 4) for kb in range(tb) for p in range(pairs[tb])]
    while len(b_masked) % 4:
        b_masked.append(b_plain.pop(0))
    b_real = [code(3 * tb + p, 0, REAL) for tb in range(4) for p in range(pairs[tb])]
    b_far = [code(3 * tb + p, kb, FREE) for tb in range(4) for kb in range(1, 4) for p in range(pairs[tb])]
    while len(b_real) % 4:
        b_real.append(b_far.pop(0))
    foreign = []
    for tb in (2, 0, 1):
        run = [code(12 + tb, 0, REAL)] + [code(12 + tb, kb, FREE) for kb in range(1, 4 + tb)] + [code(12 + tb, 4 + tb, TRI)]
        foreign.append(run + [code(12 + tb, 4 + tb, NONE)] * (len(run) % 2))
    return a_masked, a_plain, b_masked, b_plain, b_real, b_far, foreign


def lookup(i, values):
    if len(values) == 1:
        return values[0]
    if all(v == values[0] for v in values):
        return values[0]
    half = len(values) // 2
    return jnp.where(i < half, lookup(i, values[:half]), lookup(i - half, values[half:]))


def flash_run(n, unroll, code_fn, biased, me_c, q_buf, kv, vt, acc, m_s, l_s, s_buf, p_buf, top_s, decay_s, bias):
    def fields(i):
        code = code_fn(i)
        return code // 64, lax.rem(code // 8, 8), lax.rem(code, 8)

    def scores(i, slot):
        st, kb, b = fields(i)
        tb = st // 3
        own = st < 12
        place = jnp.where(own, jnp.where(tb // 2 == me_c, me_c, 2), 3)
        entry = jnp.where(own, lax.rem(tb, 2) * 3 + lax.rem(st, 3), st - 12)
        k_off = pl.multiple_of(lax.rem(kb, 2) * QB, QB)
        for u in range(2):
            q_blk = q_buf[place, entry, u]
            top = jnp.full((8, QB), NEG, jnp.float32)
            for k0 in range(0, QB, KC):
                k_blk = kv[kb // 2, me_c, 0, pl.ds(k_off + k0, KC), :]
                s = lax.dot_general(k_blk, q_blk, (((1,), (1,)), ((), ())), preferred_element_type=jnp.float32)
                if biased:
                    s = s + bias[b, k0:k0 + KC, :]
                s_buf[slot, u, k0:k0 + KC, :] = s
                top = jnp.maximum(top, jnp.max(s.reshape(KC // 8, 8, QB), axis=0))
                yield
            top_s[slot, u] = top

    def weights(i, slot):
        st = fields(i)[0]
        for u in range(2):
            m_prev = m_s[st, u]
            m_new = jnp.maximum(m_prev, jnp.max(top_s[slot, u], axis=0, keepdims=True))
            m8 = jnp.broadcast_to(m_new, (8, QB))
            total = jnp.zeros((8, QB), jnp.float32)
            for k0 in range(0, QB, PC):
                s = s_buf[slot, u, k0:k0 + PC, :].reshape(PC // 8, 8, QB)
                p = jnp.exp2((s - m8[None]) * SCALE_LOG2E)
                total = total + jnp.sum(p, axis=0)
                p_buf[slot, u, k0:k0 + PC, :] = p.reshape(PC, QB).astype(jnp.bfloat16)
                if (k0 + PC) % KC == 0:
                    yield
            decay = jnp.exp2((m_prev - m_new) * SCALE_LOG2E)
            decay_s[slot, u] = decay
            l_s[st, u] = l_s[st, u] * decay + jnp.sum(total, axis=0, keepdims=True)
            m_s[st, u] = m_new

    def values(i, slot):
        st, kb, _ = fields(i)
        k_off = pl.multiple_of(lax.rem(kb, 2) * QB, QB)
        for u in range(2):
            pv = jnp.dot(vt[kb // 2, :, pl.ds(k_off, QB)], p_buf[slot, u], preferred_element_type=jnp.float32)
            acc[st, u] = acc[st, u] * decay_s[slot, u] + pv
            for _ in range(QB // KC):
                yield

    def together(*parts):
        for _ in itertools.zip_longest(*parts):
            pass

    @pl.when(n > 0)
    def _():
        p_buf[1] = jnp.zeros_like(p_buf[1])
        decay_s[1] = jnp.ones_like(decay_s[1])
        together(scores(0, 0))

        def step(j, _):
            i = j * unroll
            for k in range(unroll):
                slot = k % 2
                prev = jnp.maximum(i - 1, 0) if k == 0 else i + k - 1
                nxt = jnp.minimum(i + k + 1, n - 1) if k == unroll - 1 else i + k + 1
                together(weights(i + k, slot), scores(nxt, 1 - slot), values(prev, 1 - slot))
            return 0

        lax.fori_loop(0, n // unroll, step, 0)
        together(values(n - 1, 1))


def attn_kernel(pos_ref, freq_ref, x_ref, gain_ref, wq_ref, wk_ref, wv_ref, out_ref, kc_ref, vc_ref,
                cos_s, sin_s, h_buf, q_buf, kv, vt, acc, m_s, l_s, s_buf, p_buf, top_s, decay_s, bias, o_buf,
                send_sem, recv_sem, qsend_sem, qrecv_sem, osend_sem, orecv_sem, cache_sem, ocopy_sem):
    me = lax.axis_index("sp")
    x = me // 2
    c = lax.rem(me, 2)
    partner = 2 * x + (1 - c)
    cross = 2 * (1 - x) + c
    diag = 2 * (1 - x) + (1 - c)
    pad = me * ROWS + (ROWS - 1) - pos_ref[ROWS - 1]
    a_masked, a_plain, b_masked, b_plain, b_real, b_far, foreign = schedules()

    barrier = pltpu.get_barrier_semaphore()
    for peer in (partner, cross, diag):
        pl.semaphore_signal(barrier, inc=1, device_id={"sp": peer}, device_id_type=MESH)

    gain = gain_ref[...].reshape(1, DIM).astype(jnp.float32)
    lane = lax.broadcasted_iota(jnp.int32, (256, 128), 1)

    def angle_rows(r):
        rows = pl.ds(r * 256, 256)
        row = lax.broadcasted_iota(jnp.int32, (256, 128), 0) + (me * ROWS + r * 256 - pad)
        ang = jnp.maximum(row, -1).astype(jnp.float32) * freq_ref[...]
        turns = jnp.floor(ang * 0.6366197723675814 + 0.5)
        red = ((ang - turns * 1.5703125) - turns * 4.837512969970703125e-4) - turns * 7.54978995489188216e-8
        sq = red * red
        sin_p = ((-1.9515295891e-4 * sq + 8.3321608736e-3) * sq - 1.6666654611e-1) * sq * red + red
        cos_p = ((2.443315711809948e-5 * sq - 1.388731625493765e-3) * sq + 4.166664568298827e-2) * sq * sq - 0.5 * sq + 1.0
        quad = (turns.astype(jnp.int32) + jnp.where(lane < 64, 0, 3)) & 3
        val = jnp.where((quad & 1) == 0, cos_p, sin_p)
        val = jnp.where((quad == 1) | (quad == 2), -val, val)
        swapped = pltpu.roll(val, 64, 1)
        cos_s[rows, :] = jnp.where(lane < 64, val, swapped)
        sin_s[rows, :] = jnp.where(lane < 64, -swapped, val)

    def rope(t, rows):
        return (t * cos_s[rows, :] + pltpu.roll(t, 64, 1) * sin_s[rows, :]).astype(jnp.bfloat16)

    for r in range(ROWS // 256):
        rows = pl.ds(r * 256, 256)
        angle_rows(r)
        xf = x_ref[rows, :].astype(jnp.float32)
        ms = jnp.mean(xf * xf, axis=-1, keepdims=True)
        h = (xf * lax.rsqrt(ms + NORM_EPS) * gain).astype(jnp.bfloat16)
        h_buf[rows, :] = h
        k = jnp.dot(h, wk_ref[...], preferred_element_type=jnp.float32)
        v = jnp.dot(h, wv_ref[...], preferred_element_type=jnp.float32).astype(jnp.bfloat16)
        for g in range(2):
            kv[me, g, 0, rows, :] = rope(k[:, g * 128:(g + 1) * 128], rows)
            kv[me, g, 1, rows, :] = v[:, g * 128:(g + 1) * 128]

    pl.semaphore_wait(barrier, 3)

    def kv_copy(src, i, peer):
        return pltpu.make_async_remote_copy(src_ref=kv.at[src], dst_ref=kv.at[src], send_sem=send_sem.at[i], recv_sem=recv_sem.at[i],
                                            device_id={"sp": peer}, device_id_type=MESH)

    to_cross = kv_copy(me, 0, cross)
    to_cross.start()
    to_partner = kv_copy(me, 1, partner)
    to_partner.start()

    def q_rows(t):
        def body(r, _):
            rows = pl.ds(pl.multiple_of(t * QB + r * 256, 256), 256)
            inner = pl.ds(pl.multiple_of(r * 256, 256), 256)
            q = jnp.dot(h_buf[rows, :], wq_ref[...], preferred_element_type=jnp.float32)
            for h in range(12):
                q_buf[h // 6, t * 3 + (h % 6) // 2, h % 2, inner, :] = rope(q[:, h * 128:(h + 1) * 128], rows)
            return 0

        lax.fori_loop(0, 2, body, 0)

    def foreign_q(t, g, peer):
        ft = 2 * c + t
        return pltpu.make_async_remote_copy(src_ref=q_buf.at[g, t * 3 + 2], dst_ref=q_buf.at[3, ft], send_sem=qsend_sem.at[t, g],
                                            recv_sem=qrecv_sem.at[ft], device_id={"sp": peer}, device_id_type=MESH)

    def send_foreign(t):
        @pl.when((x == 1) & (2 * c + t < FOREIGN))
        def _():
            foreign_q(t, c, cross).start()
            foreign_q(t, 1 - c, diag).start()

    q_rows(0)
    send_foreign(0)
    q_rows(1)
    send_foreign(1)
    q_copy = pltpu.make_async_remote_copy(src_ref=q_buf.at[1 - c], dst_ref=q_buf.at[2], send_sem=send_sem.at[3], recv_sem=recv_sem.at[3],
                                          device_id={"sp": partner}, device_id_type=MESH)
    q_copy.start()

    def flip(src):
        vt[src] = kv[src, c, 1].T

    def cache_copy(src, i):
        rows = pl.ds(pl.multiple_of(src * ROWS, ROWS), ROWS)
        return (pltpu.make_async_copy(kv.at[src, x, 0], kc_ref.at[rows, :], cache_sem.at[i, 0]),
                pltpu.make_async_copy(kv.at[src, x, 1], vc_ref.at[rows, :], cache_sem.at[i, 1]))

    for cp in cache_copy(me, 0):
        cp.start()
    flip(me)
    tri = lax.broadcasted_iota(jnp.int32, (QB, QB), 0) <= lax.broadcasted_iota(jnp.int32, (QB, QB), 1)
    real = lax.broadcasted_iota(jnp.int32, (QB, QB), 0) >= pad
    bias[TRI] = jnp.where(tri, 0.0, NEG)
    bias[REAL] = jnp.where(real, 0.0, NEG)
    bias[BOTH] = jnp.where(tri & real, 0.0, NEG)
    bias[NONE] = jnp.full((QB, QB), NEG, jnp.float32)
    bias[FREE] = jnp.zeros((QB, QB), jnp.float32)
    m_s[...] = jnp.full_like(m_s, NEG)
    l_s[...] = jnp.zeros_like(l_s)
    acc[...] = jnp.zeros_like(acc)
    to_partner.wait_recv()
    for cp in cache_copy(partner, 1):
        cp.start()
    flip(partner)
    q_copy.wait_recv()

    def flash(n, unroll, code_fn, biased):
        flash_run(n, unroll, code_fn, biased, c, q_buf, kv, vt, acc, m_s, l_s, s_buf, p_buf, top_s, decay_s, bias)

    def by_chip(a, b):
        return jnp.where(x == 0, a, b)

    flash(by_chip(len(a_masked), len(b_masked)), 4, lambda i: by_chip(lookup(i, a_masked), lookup(i, b_masked)), True)
    flash(by_chip(len(a_plain), len(b_plain)), 4, lambda i: by_chip(lookup(i, a_plain), lookup(i, b_plain)), False)

    def o_place(t, col):
        return out_ref.at[pl.ds(pl.multiple_of(t * QB, QB), QB), pl.ds(pl.multiple_of(col * 256, 256), 256)]

    def o_send(st, t, col, peer):
        return pltpu.make_async_remote_copy(src_ref=o_buf.at[st], dst_ref=o_place(t, col), send_sem=osend_sem.at[st], recv_sem=orecv_sem.at[t, col],
                                            device_id={"sp": peer}, device_id_type=MESH)

    def o_keep(st, t, col):
        return pltpu.make_async_copy(o_buf.at[st], o_place(t, col), ocopy_sem.at[t, lax.rem(col, 3)])

    def finish(st):
        q_idx = lax.broadcasted_iota(jnp.int32, (1, QB), 1) + (x * 2 * ROWS + (st // 3) * QB)
        for u in range(2):
            inv = jnp.where(q_idx >= pad, 1.0 / l_s[st, u], 0.0)
            o_buf[st, :, u * 128:(u + 1) * 128] = (acc[st, u] * inv).T.astype(jnp.bfloat16)

    def here(tb, pair):
        return (x == 0) | (pair < 2) | (tb >= FOREIGN)

    def finish_own(j, _):
        half = jnp.where(j < 6, 1 - c, c)
        t = lax.rem(j, 6) // 3
        pair = lax.rem(j, 3)
        tb = 2 * half + t
        st = 3 * tb + pair

        @pl.when(here(tb, pair))
        def _():
            finish(st)

            @pl.when(j < 6)
            def _():
                o_send(st, t, 3 * c + pair, partner).start()

            @pl.when(j >= 6)
            def _():
                o_keep(st, t, 3 * c + pair).start()

        return 0

    @pl.when(x == 0)
    def _():
        lax.fori_loop(0, 12, finish_own, 0)

    to_cross.wait_recv()
    forward = kv_copy(cross, 2, partner)
    forward.start()
    for cp in cache_copy(cross, 2):
        cp.start()
    flip(cross)
    kv_copy(diag, 2, partner).wait_recv()
    for cp in cache_copy(diag, 3):
        cp.start()
    flip(diag)

    f_len = [len(run) for run in foreign]
    f_all = sum(foreign, [])
    f_tb = [2, 0, 1]

    def far_round(j, _):
        ft = lookup(j, f_tb)

        @pl.when(x == 0)
        def _():
            pltpu.make_async_remote_copy(src_ref=q_buf.at[0, 2], dst_ref=q_buf.at[3, ft], send_sem=qsend_sem.at[0, 0],
                                         recv_sem=qrecv_sem.at[ft], device_id={"sp": cross}, device_id_type=MESH).wait_recv()

        start = lookup(j, [sum(f_len[:k]) for k in range(FOREIGN)])
        flash(by_chip(lookup(j, f_len), len(b_real)), 2, lambda i: by_chip(lookup(i + start, f_all), lookup(i, b_real)), True)

        @pl.when(x == 0)
        def _():
            finish(12 + ft)
            o_send(12 + ft, lax.rem(ft, 2), 3 * c + 2, 2 + ft // 2).start()

        return 0

    lax.fori_loop(0, by_chip(FOREIGN, 1), far_round, 0)
    flash(by_chip(0, len(b_far)), 4, lambda i: lookup(i, b_far), False)

    @pl.when(x == 1)
    def _():
        lax.fori_loop(0, 12, finish_own, 0)

    to_cross.wait_send()
    to_partner.wait_send()
    forward.wait_send()
    q_copy.wait_send()
    for i, src in enumerate((me, partner, cross, diag)):
        for cp in cache_copy(src, i):
            cp.wait()
    for t in range(2):
        @pl.when((x == 1) & (2 * c + t < FOREIGN))
        def _():
            foreign_q(t, c, cross).wait_send()
            foreign_q(t, 1 - c, diag).wait_send()

        for pair in range(3):
            mine = here(2 * c + t, pair)
            theirs = here(2 * (1 - c) + t, pair)

            @pl.when(mine)
            def _():
                o_keep(0, t, 3 * c + pair).wait()

            @pl.when(jnp.logical_not(mine))
            def _():
                o_send(0, t, 3 * c + pair, cross).wait_recv()

            o_send(0, t, 3 * (1 - c) + pair, partner).wait_recv()

            @pl.when(theirs)
            def _():
                o_send(3 * (2 * (1 - c) + t) + pair, t, 3 * c + pair, partner).wait_send()

    @pl.when(x == 0)
    def _():
        for ft in range(FOREIGN):
            o_send(12 + ft, ft % 2, 3 * c + 2, 2 + ft // 2).wait_send()


def attn_call(positions, freq, x, gain, w_query, w_key, w_value):
    vm = pl.BlockSpec(memory_space=pltpu.VMEM)
    hbm = pl.BlockSpec(memory_space=pl.ANY)
    flops = 2 * ROWS * DIM * 2048 + 4 * 128 * 3 * 4096 * 2048
    bf, f32 = jnp.bfloat16, jnp.float32
    dma = pltpu.SemaphoreType.DMA
    return pl.pallas_call(
        attn_kernel,
        out_shape=(jax.ShapeDtypeStruct((ROWS, DIM), bf), jax.ShapeDtypeStruct((4 * ROWS, 128), bf), jax.ShapeDtypeStruct((4 * ROWS, 128), bf)),
        in_specs=[pl.BlockSpec(memory_space=pltpu.SMEM)] + [vm] * 6,
        out_specs=(hbm, hbm, hbm),
        scratch_shapes=[
            pltpu.VMEM((ROWS, 128), f32),
            pltpu.VMEM((ROWS, 128), f32),
            pltpu.VMEM((ROWS, DIM), bf),
            pltpu.VMEM((4, 6, 2, QB, 128), bf),
            pltpu.VMEM((4, 2, 2, ROWS, 128), bf),
            pltpu.VMEM((4, 128, ROWS), bf),
            pltpu.VMEM((12 + FOREIGN, 2, 128, QB), f32),
            pltpu.VMEM((12 + FOREIGN, 2, 1, QB), f32),
            pltpu.VMEM((12 + FOREIGN, 2, 1, QB), f32),
            pltpu.VMEM((2, 2, QB, QB), f32),
            pltpu.VMEM((2, 2, QB, QB), bf),
            pltpu.VMEM((2, 2, 8, QB), f32),
            pltpu.VMEM((2, 2, 1, QB), f32),
            pltpu.VMEM((5, QB, QB), f32),
            pltpu.VMEM((12 + FOREIGN, QB, 256), bf),
            dma((4,)), dma((4,)), dma((2, 2)), dma((FOREIGN,)), dma((12 + FOREIGN,)), dma((2, 6)), dma((4, 2)), dma((2, 3)),
        ],
        compiler_params=pltpu.CompilerParams(vmem_limit_bytes=62 << 20, collective_id=0, has_side_effects=True),
        cost_estimate=pl.CostEstimate(flops=flops, bytes_accessed=20 << 20, transcendentals=3 * 4096 * 2048),
        name="attn_block",
    )(positions, freq, x, gain, w_query, w_key, w_value)


def solution(mesh):
    freq = 1.0 / (ROPE_THETA ** (np.arange(0, HEAD_DIM, 2, dtype=np.float64) / HEAD_DIM))
    freq = np.concatenate([freq, freq]).astype(np.float32).reshape(1, HEAD_DIM)

    def layer_shard(hidden, positions, attn_gain, w_query, w_key, w_value, w_out, mlp_gain, w_gate, w_up, w_down):
        attn, k_all, v_all = attn_call(positions, jnp.asarray(freq), hidden, attn_gain, w_query, w_key, w_value)
        hidden_out, k_cache, v_cache = mlp_call(attn, hidden, w_out, mlp_gain, w_gate, w_up, w_down, k_all, v_all)
        return hidden_out, k_cache.reshape(4 * ROWS, 1, HEAD_DIM), v_cache.reshape(4 * ROWS, 1, HEAD_DIM)

    row_spec = P(("dp", "sp"), None)
    cache_spec = P("dp", "sp", None)
    return jax.shard_map(layer_shard, mesh=mesh, in_specs=(row_spec, P(("dp", "sp")), P(), P(), P(), P(), P(), P(), P(), P(), P()), out_specs=(row_spec, cache_spec, cache_spec), check_vma=False)
```

time: 197 us -> 177 us (0.90)
  the two profiles are of different devices: /device:TPU:7 before, /device:TPU:0 now
where the time goes in v4:
time: 177 us
  Pallas kernels  176 us (99%)
    pallas_call x1, Pallas kernels, mlp_call(): pl.pallas_call(functools.partial(mlp_kernel, fb, rt), out_shape=(jax.Shap...  101 us
    pallas_call x1, Pallas kernels, attn_call(): pl.pallas_call(attn_kernel, out_shape=(jax.ShapeDtypeStruct((ROWS, DIM),...  75.8 us

profile of v4, /device:TPU:0, one launch (start us, length us, event | category | flops | bytes accessed | tf_op | source)
XLA Modules:
  0.0 177.2 jit_solution(5206103526654480957)
XLA Ops:
  0.6 75.8 %attn_block.1 = (bf16[1024,1536]{1,0:T(8,128)(2,1)}, bf16[4096,128]{1,0:T(8,128)(2,1)}, bf16[4096,128]{1,0:T(8,128)(2,1)}) custom-call(s32[1024]{0:T(1024)} %pos_ref.1, f32[1,128]{1,0:T(1,128)} %constant.2.clone.freq_ref, bf16[1024,1536]{1,0:T(8,128)(2,1)} %x_ref.3, bf16[1536]{0:T(1024)(128)(2,1)} %gain_ref.2, bf16[1536,1536]{1,0:T(8,128)(2,1)} %wq_ref.1, ...), custom_call_target="tpu_custom_call" | custom-call | flops 19327352832 | bytes 20971520 | tf_op jit(solution)/shard_map/attn_block/pallas_call | solution.py:488
  76.5 100.5 %mlp_block.1 = (bf16[1024,1536]{1,0:T(8,128)(2,1)}, bf16[4096,128]{1,0:T(8,128)(2,1)}, bf16[4096,128]{1,0:T(8,128)(2,1)}) custom-call(bf16[1024,1536]{1,0:T(8,128)(2,1)} %get-tuple-element.9.o_ref, bf16[1024,1536]{1,0:T(8,128)(2,1)} %x_ref.3, bf16[1536,1536]{1,0:T(8,128)(2,1)} %wout_ref.1, bf16[1536]{0:T(1024)(128)(2,1)} %gain_ref.3, ...), custom_call_target="tpu_custom_call" | custom-call | flops 89389006848 | bytes 82575360 | tf_op jit(solution)/shard_map/mlp_block/pallas_call | solution.py:89
